TPU v7x, 128 devices: a whole 4x4x4 slice. The times are simulated.
128 devices in a mesh: col: 2 (over core), row: 64 (over z, y, x).
Axes of the slice: x: 4, y: 4, z: 4, core: 2. Of those that a mesh axis runs over, the one named last changes fastest.
Arguments:
- inter_mask: int32 [32768, 8192], P('row', 'col')
- user_emb: bfloat16 [32768, 64], P(('row', 'col'))
- item_emb: bfloat16 [8192, 64], P(('col', 'row'))
- triples: int32 [2048, 3], replicated
Outputs:
- output 1: bfloat16 [32768, 64], P(('row', 'col'))
- output 2: bfloat16 [8192, 64], P(('col', 'row'))
- output 3: float32 [], replicated
- output 4: float32 [32768, 64], P(('row', 'col'))
- output 5: float32 [8192, 64], P(('col', 'row'))
All inputs are finite; a program needn't handle non-finite values.
Results may differ from a plain program's by a relative error of at most 0.0191124.
Values are sent between devices in bfloat16 or wider.
A program may use at most 1 GiB of HBM per device.

v0:
```python
import jax
import jax.numpy as jnp
from jax import lax
from jax.sharding import PartitionSpec as P, NamedSharding

LAYERS = 3


def solution(mesh):
    n_col = mesh.shape['col']
    n_row = mesh.shape['row']

    def local_fn(mask_blk, user_emb, item_emb, triples):
        row_idx = lax.axis_index('row')
        col_idx = lax.axis_index('col')
        user_rows = user_emb.shape[0]
        item_rows = item_emb.shape[0]
        n_batch = triples.shape[0]

        deg_user = jnp.maximum(lax.psum(jnp.sum(mask_blk, axis=1, dtype=jnp.int32), 'col'), 1)
        deg_item = jnp.maximum(lax.psum(jnp.sum(mask_blk, axis=0, dtype=jnp.int32), 'row'), 1)
        scale_user = lax.rsqrt(deg_user.astype(jnp.float32))
        scale_item = lax.rsqrt(deg_item.astype(jnp.float32))
        adj_blk = (scale_user[:, None] * mask_blk.astype(jnp.float32) * scale_item[None, :]).astype(jnp.bfloat16)

        def user_half(item_shard):
            gathered = lax.all_gather(item_shard, 'row', axis=0, tiled=True)
            partial_sum = jnp.dot(adj_blk, gathered, preferred_element_type=jnp.float32)
            return lax.psum_scatter(partial_sum, 'col', scatter_dimension=0, tiled=True)

        def item_half(user_shard):
            gathered = lax.all_gather(user_shard, 'col', axis=0, tiled=True)
            partial_sum = lax.dot_general(adj_blk, gathered, (((0,), (0,)), ((), ())), preferred_element_type=jnp.float32)
            return lax.psum_scatter(partial_sum, 'row', scatter_dimension=0, tiled=True)

        user_cur = user_emb
        item_cur = item_emb
        user_acc = user_emb.astype(jnp.float32)
        item_acc = item_emb.astype(jnp.float32)
        for _ in range(LAYERS):
            user_next = user_half(item_cur).astype(jnp.bfloat16)
            item_next = item_half(user_cur).astype(jnp.bfloat16)
            user_acc = user_acc + user_next.astype(jnp.float32)
            item_acc = item_acc + item_next.astype(jnp.float32)
            user_cur, item_cur = user_next, item_next
        user_final = (user_acc / (LAYERS + 1)).astype(jnp.bfloat16)
        item_final = (item_acc / (LAYERS + 1)).astype(jnp.bfloat16)

        user_base = (row_idx * n_col + col_idx) * user_rows
        item_base = (col_idx * n_row + row_idx) * item_rows
        local_user = triples[:, 0] - user_base
        local_pos = triples[:, 1] - item_base
        local_neg = triples[:, 2] - item_base

        def lookup_rows(emb_table, local_ids):
            is_owned = (local_ids >= 0) & (local_ids < emb_table.shape[0])
            picked = jnp.take(emb_table, jnp.clip(local_ids, 0, emb_table.shape[0] - 1), axis=0).astype(jnp.float32)
            seg_ids = jnp.where(is_owned, local_ids, emb_table.shape[0])
            return jnp.where(is_owned[:, None], picked, 0.0), seg_ids

        rows_user, seg_user = lookup_rows(user_final, local_user)
        rows_pos, seg_pos = lookup_rows(item_final, local_pos)
        rows_neg, seg_neg = lookup_rows(item_final, local_neg)
        fetched = lax.psum(jnp.concatenate([rows_user, rows_pos, rows_neg], axis=0), ('row', 'col'))
        e_user = fetched[:n_batch]
        e_pos = fetched[n_batch:2 * n_batch]
        e_neg = fetched[2 * n_batch:]
        margin = jnp.sum(e_user * e_pos, axis=1) - jnp.sum(e_user * e_neg, axis=1)
        bpr_loss = jnp.mean(jax.nn.softplus(-margin))
        loss_coef = -jax.nn.sigmoid(-margin) / n_batch
        grad_eu = loss_coef[:, None] * (e_pos - e_neg)
        grad_epos = loss_coef[:, None] * e_user
        seed_user = jax.ops.segment_sum(grad_eu, seg_user, num_segments=user_rows)
        seed_item = jax.ops.segment_sum(jnp.concatenate([grad_epos, -grad_epos], axis=0), jnp.concatenate([seg_pos, seg_neg], axis=0), num_segments=item_rows)

        src_user = seed_user / (LAYERS + 1)
        src_item = seed_item / (LAYERS + 1)
        cot_user = src_user.astype(jnp.bfloat16)
        cot_item = src_item.astype(jnp.bfloat16)
        for _ in range(LAYERS - 1):
            new_user = (src_user + user_half(cot_item)).astype(jnp.bfloat16)
            new_item = (src_item + item_half(cot_user)).astype(jnp.bfloat16)
            cot_user, cot_item = new_user, new_item
        grad_user = src_user + user_half(cot_item)
        grad_item = src_item + item_half(cot_user)
        return user_final, item_final, bpr_loss, grad_user, grad_item

    user_spec = P(('row', 'col'), None)
    item_spec = P(('col', 'row'), None)
    return jax.shard_map(local_fn, mesh=mesh, in_specs=(P('row', 'col'), user_spec, item_spec, P()), out_specs=(user_spec, item_spec, P(), user_spec, item_spec), check_vma=False)
```

profile of v0, /device:TPU:0, one launch (start us, length us, event | category | flops | bytes accessed | tf_op | source)
XLA Modules:
  0.0 3855.7 jit_solution(7874639667352506075)
XLA Ops:
  11.3 350.3 %psum.22 = s32[4096]{0:T(1024)S(1)} all-reduce(s32[4096]{0:T(1024)S(1)} %get-tuple-element.7), channel_id=1, replica_groups=mesh['col'=2,'row'=64] {'row'}, use_global_device_ids=true, to_apply=%region_3.0 | all-reduce | flops 4096 | bytes 32768 | tf_op jit(solution)/shard_map/psum | solution.py:21
  363.4 175.0 %all_gather.36 = bf16[4096,64]{1,0:T(8,128)(2,1)S(1)} all-gather(bf16[64,64]{1,0:T(8,128)(2,1)S(1)} %copy-done.8), channel_id=1, replica_groups=mesh['col'=2,'row'=64] {'row'}, dimensions={0}, use_global_device_ids=true | all-gather | bytes 532480 | tf_op jit(solution)/shard_map/all_gather | solution.py:27
  538.4 4.8 multiply_convert_fusion
  549.2 4.8 fusion.19
  556.8 357.1 %reduce-scatter.15.cloned.1.call-done = f32[64,64]{1,0:T(8,128)} async-done(((f32[4096,64]{1,0:T(8,128)}), f32[64,64]{1,0:T(8,128)}) %reduce-scatter.15.cloned.1.call-update) | async-done | bytes 16400 | tf_op jit(solution)/shard_map/reduce_scatter | solution.py:34
  914.6 175.8 %all_gather.38 = bf16[4096,64]{1,0:T(8,128)(2,1)S(1)} all-gather(bf16[64,64]{1,0:T(8,128)(2,1)S(1)} %convert_element_type.94), channel_id=1, replica_groups=mesh['col'=2,'row'=64] {'row'}, dimensions={0}, use_global_device_ids=true | all-gather | bytes 532480 | tf_op jit(solution)/shard_map/all_gather | solution.py:27
  1102.3 4.8 fusion.23
  1107.5 352.7 %reduce-scatter.19.cloned.1.call-done = f32[64,64]{1,0:T(8,128)} async-done(((f32[4096,64]{1,0:T(8,128)}), f32[64,64]{1,0:T(8,128)}) %reduce-scatter.19.cloned.1.call-update) | async-done | bytes 16400 | tf_op jit(solution)/shard_map/reduce_scatter | solution.py:34
  1460.2 354.3 %reduce-scatter.23.cloned.1.call-done = f32[64,64]{1,0:T(8,128)} async-done(((f32[4096,64]{1,0:T(8,128)}), f32[64,64]{1,0:T(8,128)}) %reduce-scatter.23.cloned.1.call-update) | async-done | bytes 16400 | tf_op jit(solution)/shard_map/reduce_scatter | solution.py:34
  1815.3 6.2 gather_fusion.1
  1821.5 6.2 gather_fusion.2
  1827.7 175.7 %all_gather.40 = bf16[4096,64]{1,0:T(8,128)(2,1)S(1)} all-gather(bf16[64,64]{1,0:T(8,128)(2,1)S(1)} %get-tuple-element.19), channel_id=1, replica_groups=mesh['col'=2,'row'=64] {'row'}, dimensions={0}, use_global_device_ids=true | all-gather | bytes 532480 | tf_op jit(solution)/shard_map/all_gather | solution.py:27
  2013.3 6.2 gather_fusion
  2022.2 155.3 %all-reduce.2.cloned.1.call-done = f32[6144,64]{1,0:T(8,128)} async-done(((f32[6144,64]{1,0:T(8,128)}), f32[6144,64]{1,0:T(8,128)}) %all-reduce.2.cloned.1.call-update) | async-done | bytes 1572880 | tf_op jit(solution)/shard_map/psum | solution.py:64
  2182.1 23.5 scatter_custom_fusion.1
  2205.7 178.9 %all_gather.42 = bf16[4096,64]{1,0:T(8,128)(2,1)S(1)} all-gather(bf16[64,64]{1,0:T(8,128)(2,1)S(1)} %multiply_convert_fusion.4), channel_id=1, replica_groups=mesh['col'=2,'row'=64] {'row'}, dimensions={0}, use_global_device_ids=true | all-gather | bytes 532480 | tf_op jit(solution)/shard_map/all_gather | solution.py:27
  2389.0 12.5 scatter_custom_fusion
  2404.3 4.8 fusion.25
  2411.1 4.8 fusion.27
  2415.9 344.1 %reduce-scatter.27.cloned.1.call-done = f32[64,64]{1,0:T(8,128)} async-done(((f32[4096,64]{1,0:T(8,128)}), f32[64,64]{1,0:T(8,128)}) %reduce-scatter.27.cloned.1.call-update) | async-done | bytes 16400 | tf_op jit(solution)/shard_map/reduce_scatter | solution.py:34
  2760.1 354.4 %reduce-scatter.31.cloned.1.call-done = f32[64,64]{1,0:T(8,128)} async-done(((f32[4096,64]{1,0:T(8,128)}), f32[64,64]{1,0:T(8,128)}) %reduce-scatter.31.cloned.1.call-update) | async-done | bytes 16400 | tf_op jit(solution)/shard_map/reduce_scatter | solution.py:34
  3115.3 175.9 %all_gather.44 = bf16[4096,64]{1,0:T(8,128)(2,1)S(1)} all-gather(bf16[64,64]{1,0:T(8,128)(2,1)S(1)} %get-tuple-element.25), channel_id=1, replica_groups=mesh['col'=2,'row'=64] {'row'}, dimensions={0}, use_global_device_ids=true | all-gather | bytes 532480 | tf_op jit(solution)/shard_map/all_gather | solution.py:27
  3295.4 176.0 %all_gather.46 = bf16[4096,64]{1,0:T(8,128)(2,1)S(1)} all-gather(bf16[64,64]{1,0:T(8,128)(2,1)S(1)} %get-tuple-element.24), channel_id=1, replica_groups=mesh['col'=2,'row'=64] {'row'}, dimensions={0}, use_global_device_ids=true | all-gather | bytes 532480 | tf_op jit(solution)/shard_map/all_gather | solution.py:27
  3489.1 357.6 %reduce-scatter.35.cloned.1.call-done = f32[64,64]{1,0:T(8,128)} async-done(((f32[4096,64]{1,0:T(8,128)}), f32[64,64]{1,0:T(8,128)}) %reduce-scatter.35.cloned.1.call-update) | async-done | bytes 16400 | tf_op jit(solution)/shard_map/reduce_scatter | solution.py:34
  (96 shorter events, 78.1 us)
Async XLA Ops:
  7.2 356.2 %copy-start.8 = (bf16[64,64]{1,0:T(8,128)(2,1)S(1)}, bf16[64,64]{1,0:T(8,128)(2,1)}, u32[]{:S(2)}) copy-start(bf16[64,64]{1,0:T(8,128)(2,1)} %param.8) | copy-start | bytes 24580
  7.2 546.9 %reduce-scatter.13.cloned.1.call-start = ((), (), s32[]{:S(2)}) async-start(), calls=%async_computation.12 | async-start | bytes 196608 | tf_op jit(solution)/shard_map/reduce_scatter | solution.py:29
  543.3 1.9 copy-start.1
  545.2 2.1 copy-start.6
  547.2 366.6 %reduce-scatter.15.cloned.1.call-start = ((), (), s32[]{:S(2)}) async-start(), calls=%async_computation.13 | async-start | bytes 2129920 | tf_op jit(solution)/shard_map/reduce_scatter | solution.py:34
  554.0 545.6 %reduce-scatter.17.cloned.1.call-start = ((), (), s32[]{:S(2)}) async-start(), calls=%async_computation.14 | async-start | bytes 196608 | tf_op jit(solution)/shard_map/reduce_scatter | solution.py:29
  1094.7 365.5 %reduce-scatter.19.cloned.1.call-start = ((), (), s32[]{:S(2)}) async-start(), calls=%async_computation.15 | async-start | bytes 2129920 | tf_op jit(solution)/shard_map/reduce_scatter | solution.py:34
  1099.6 714.9 %reduce-scatter.23.cloned.1.call-start = ((), (), s32[]{:S(2)}) async-start(), calls=%async_computation.17 | async-start | bytes 2129920 | tf_op jit(solution)/shard_map/reduce_scatter | solution.py:34
  1102.3 4.9 copy-start.9
  1102.3 712.2 %copy-start.5 = (f32[64,64]{1,0:T(8,128)S(1)}, f32[64,64]{1,0:T(8,128)}, u32[]{:S(2)}) copy-start(f32[64,64]{1,0:T(8,128)} %reduce-scatter.15.cloned.1.call-done) | copy-start | bytes 49156
  1107.2 905.1 %reduce-scatter.21.cloned.1.call-start = ((), (), s32[]{:S(2)}) async-start(), calls=%async_computation.16 | async-start | bytes 196608 | tf_op jit(solution)/shard_map/reduce_scatter | solution.py:29
  1815.3 12.4 copy-start
  2003.4 8.9 copy-start.3
  2003.4 8.9 copy-start.4
  2007.7 169.8 %all-reduce.2.cloned.1.call-start = ((), (), s32[]{:S(2)}) async-start(), calls=%async_computation.18 | async-start | bytes 6291456 | tf_op jit(solution)/shard_map/psum | solution.py:64
  2013.1 9.0 copy-start.7
  2022.2 379.4 %reduce-scatter.25.cloned.1.call-start = ((), (), s32[]{:S(2)}) async-start(), calls=%async_computation.19 | async-start | bytes 196608 | tf_op jit(solution)/shard_map/reduce_scatter | solution.py:29
  2205.7 183.3 %copy-start.2 = (f32[6144,64]{1,0:T(8,128)S(1)}, f32[6144,64]{1,0:T(8,128)}, u32[]{:S(2)}) copy-start(f32[6144,64]{1,0:T(8,128)} %all-reduce.2.cloned.1.call-done) | copy-start | bytes 4718596
  2388.9 371.2 %reduce-scatter.27.cloned.1.call-start = ((), (), s32[]{:S(2)}) async-start(), calls=%async_computation.20 | async-start | bytes 2129920 | tf_op jit(solution)/shard_map/reduce_scatter | solution.py:34
  2409.1 705.3 %reduce-scatter.31.cloned.1.call-start = ((), (), s32[]{:S(2)}) async-start(), calls=%async_computation.22 | async-start | bytes 2129920 | tf_op jit(solution)/shard_map/reduce_scatter | solution.py:34
  2415.9 1059.8 %reduce-scatter.29.cloned.1.call-start = ((), (), s32[]{:S(2)}) async-start(), calls=%async_computation.21 | async-start | bytes 196608 | tf_op jit(solution)/shard_map/reduce_scatter | solution.py:29
  3295.4 184.8 %reduce-scatter.33.cloned.1.call-start = ((), (), s32[]{:S(2)}) async-start(), calls=%async_computation.23 | async-start | bytes 196608 | tf_op jit(solution)/shard_map/reduce_scatter | solution.py:29
  3475.7 371.0 %reduce-scatter.35.cloned.1.call-start = ((), (), s32[]{:S(2)}) async-start(), calls=%async_computation.24 | async-start | bytes 2129920 | tf_op jit(solution)/shard_map/reduce_scatter | solution.py:34
Sparse Core Ops, SparseCore 0:
  547.4 5.1 reduce-scatter.12
  554.9 358.9 reduce-scatter.14
  1094.8 4.3 reduce-scatter.16
  1101.4 358.7 reduce-scatter.18
  1462.4 352.0 reduce-scatter.22
  2007.8 4.4 reduce-scatter.20
  2022.3 155.1 all-reduce.1
  2389.0 3.4 reduce-scatter.24
  2409.3 350.7 reduce-scatter.26
  2762.3 352.1 reduce-scatter.30
  3295.5 4.2 reduce-scatter.28
  3475.8 4.3 reduce-scatter.32
  3488.6 358.0 reduce-scatter.34
where the time goes:
time: 3860 us
  waiting for transfers between devices  2280 us (59%)
  blocking collectives  1420 us (37%)
  other arithmetic  62.3 us (2%)
  matrix products  52.2 us (1%)
    reduce_scatter x6, waiting for transfers between devices, item_half(): return lax.psum_scatter(partial_sum, 'row', scatter_dimension=0, tiled=True)  2120 us
    all_gather x6, blocking collectives, user_half(): gathered = lax.all_gather(item_shard, 'row', axis=0, tiled=True)  1060 us
    psum x1, blocking collectives, local_fn(): lax.psum(jnp.sum(mask_blk, axis=0, dtype=jnp.int32), 'row')  350 us
    psum x1, waiting for transfers between devices, local_fn(): lax.psum(jnp.concatenate([rows_user, rows_pos, rows_neg], axis=0), ('row'...  155 us
  transfers between devices with their start and end apart: 13, of which 9 were waited for; matrix products, arithmetic and copies ran while one was open for 1% of the time, Pallas kernels for 0%

commit v1 on v0

v1 whole, which is shorter than its diff:
```python
import jax
import jax.numpy as jnp
from jax import lax
from jax.experimental import pallas as pl
from jax.experimental.pallas import tpu as pltpu
from jax.sharding import PartitionSpec as P

SIDE = 4
STRIDE = (16, 4, 1)
EMB = 64
CHUNK = 256
NCHUNK = 16
LAYERS = 3
STAGES = 2 * LAYERS
RS_ORDER = ((0, 1, 2), (2, 1, 0))
F32 = jnp.float32
BF16 = jnp.bfloat16
NSEM = 480
NT = (((1,), (1,)), ((), ()))
MESH = pl.DeviceIdType.MESH


def block_rows(part, q):
    return slice(32 * part + 16 * (q // 2), 32 * part + 16 * (q // 2) + 16)


def block_lanes(q):
    return slice(128 * (q % 2), 128 * (q % 2) + 128)


def join_blocks(get):
    rows = []
    for part in range(2):
        for half in range(2):
            rows.append(jnp.concatenate([get(part, 2 * half), get(part, 2 * half + 1)], axis=1))
    return jnp.concatenate(rows, axis=0)


def kernel(mask_hbm, user_ref, item_ref, ids_ref,
           fu_ref, fi_ref, loss_ref, gu_ref, gi_ref,
           mask, adj, rowsum, rowsum_in, scale_u, colsum, colsum_in, scale_i,
           ut, up, up_in, u_acc, s_user,
           nat, it, part_sum, q1, q2, r1, r2, r3, i_acc, s_item,
           fin_b, fin_f, nat_f,
           sel, sel_in, w0, w1, w2, in1, in2, in3, rows_all, grad_u, grad_i, prod_u, prod_i,
           mask_sem, send_sem, recv_sem):
    row = lax.axis_index('row')
    col = lax.axis_index('col')
    pos = (row // 16, (row // 4) % 4, row % 4)
    z, y, x = pos
    users = user_ref.shape[0]
    n_batch = ids_ref.shape[1]

    def peer(axis, k):
        return {'row': row + ((pos[axis] + k) % SIDE - pos[axis]) * STRIDE[axis]}

    partner = {'col': 1 - col}

    copies = []
    for j in range(NCHUNK):
        cp = pltpu.make_async_copy(mask_hbm.at[:, pl.ds(j * CHUNK, CHUNK)], mask.at[j], mask_sem.at[j])
        cp.start()
        copies.append(cp)

    barrier = pltpu.get_barrier_semaphore()
    for axis in range(3):
        for k in range(1, SIDE):
            pl.semaphore_signal(barrier, inc=1, device_id=peer(axis, k), device_id_type=MESH)
    pl.semaphore_signal(barrier, inc=1, device_id=partner, device_id_type=MESH)
    pl.semaphore_wait(barrier, 10)

    sent = []

    def send(src, dst, device):
        i = len(sent)
        cp = pltpu.make_async_remote_copy(src_ref=src, dst_ref=dst, send_sem=send_sem.at[i], recv_sem=recv_sem.at[i],
                                          device_id=device, device_id_type=MESH)
        cp.start()
        sent.append(cp)
        return cp

    def send_axis(axis, src, dst):
        return [send(src((pos[axis] + k) % SIDE), dst(k - 1), peer(axis, k)) for k in range(1, SIDE)]

    def arrive(cps):
        for cp in cps:
            cp.wait_recv()

    ut[0, col] = user_ref[...].astype(F32).T.astype(BF16)
    u_first = [send(ut.at[0, col], ut.at[0, col], partner)]
    nat[x] = item_ref[...]
    i_first = send_axis(2, lambda t: nat.at[x], lambda k: nat.at[x])

    rowsum[...] = jnp.zeros_like(rowsum)
    for j in range(NCHUNK):
        copies[j].wait()
        m = mask[j]
        rowsum[...] += m[:, :128] + m[:, 128:]
        s = jnp.sum(m, axis=0, keepdims=True)
        colsum[0, 2 * j:2 * j + 1, :] = s[:, :128]
        colsum[0, 2 * j + 1:2 * j + 2, :] = s[:, 128:]
    rs_cp = [send(rowsum, rowsum_in, partner)]
    cs_cp = send_axis(0, lambda t: colsum.at[0], lambda k: colsum_in.at[0, k])

    arrive(i_first)
    chunk0 = jnp.concatenate([nat[k].astype(F32) for k in range(SIDE)], axis=0).T
    for part in range(2):
        for q in range(SIDE):
            it[0, part, z, y, q] = chunk0[block_rows(part, q), block_lanes(q)].astype(BF16)

    def gather_start(s, axis):
        if axis == 2:
            ref = it.at[s, :, z, y, x]
        elif axis == 0:
            ref = it.at[s, :, z, y]
        else:
            ref = it.at[s, :, :, y]
        return send_axis(axis, lambda t: ref, lambda k: ref)

    ag = gather_start(0, 0)
    arrive(rs_cp)
    deg_u = jnp.maximum(jnp.sum(rowsum[...] + rowsum_in[...], axis=1, keepdims=True), 1)
    scale_u[...] = jnp.broadcast_to(lax.rsqrt(deg_u.astype(F32)), scale_u.shape)
    arrive(cs_cp)
    colsum[1] = colsum[0] + colsum_in[0, 0] + colsum_in[0, 1] + colsum_in[0, 2]
    cs_cp = send_axis(1, lambda t: colsum.at[1], lambda k: colsum_in.at[1, k])
    arrive(ag)
    ag = gather_start(0, 1)
    arrive(cs_cp)
    colsum[2] = colsum[1] + colsum_in[1, 0] + colsum_in[1, 1] + colsum_in[1, 2]
    cs_cp = send_axis(2, lambda t: colsum.at[2], lambda k: colsum_in.at[2, k])
    arrive(cs_cp)
    deg_i = jnp.maximum(colsum[2] + colsum_in[2, 0] + colsum_in[2, 1] + colsum_in[2, 2], 1)
    scale_i[...] = lax.rsqrt(deg_i.astype(F32))
    for j in range(NCHUNK):
        su = scale_u[...]
        m = mask[j].astype(F32)
        adj[j, :, :128] = (su * m[:, :128] * scale_i[2 * j:2 * j + 1, :]).astype(BF16)
        adj[j, :, 128:] = (su * m[:, 128:] * scale_i[2 * j + 1:2 * j + 2, :]).astype(BF16)

    def item_product(s):
        lhs = jnp.concatenate([ut[s, 0], ut[s, 1]], axis=1)

        def body(zz, _):
            for yy in range(SIDE):
                out = jnp.dot(lhs, adj[zz * SIDE + yy], preferred_element_type=F32)
                for part in range(2):
                    for q in range(SIDE):
                        part_sum[s, part, zz, yy, q] = out[block_rows(part, q), block_lanes(q)]
            return 0

        lax.fori_loop(0, SIDE, body, 0)

    def user_product(s):
        def body(zz, acc):
            for yy in range(SIDE):
                lhs = join_blocks(lambda part, q: it[s, part, zz, yy, q])
                acc = acc + lax.dot_general(lhs, adj[zz * SIDE + yy], NT, preferred_element_type=F32)
            return acc

        acc = lax.fori_loop(0, SIDE, body, jnp.zeros((EMB, 2 * users), F32))
        up[s, 0] = acc[:, :users]
        up[s, 1] = acc[:, users:]
        return [send(up.at[s], up_in.at[s], partner)]

    def at(ref, axis, t):
        return ref.at[(slice(None),) * axis + (t,)]

    def scatter_start(s):
        return [send_axis(RS_ORDER[p][0],
                          lambda t, p=p: at(part_sum.at[s, p], RS_ORDER[p][0], t),
                          lambda k, p=p: r1.at[s, p, k]) for p in range(2)]

    def scatter_mid(s, cps):
        out = []
        for p in range(2):
            a0, a1, _ = RS_ORDER[p]
            arrive(cps[p])
            q1[s, p] = at(part_sum.at[s, p], a0, pos[a0])[...] + r1[s, p, 0] + r1[s, p, 1] + r1[s, p, 2]
            rest = [a for a in range(3) if a != a0]
            out.append(send_axis(a1, lambda t, p=p: at(q1.at[s, p], rest.index(a1), t), lambda k, p=p: r2.at[s, p, k]))
        return out

    def scatter_last(s, cps):
        out = []
        for p in range(2):
            a0, a1, a2 = RS_ORDER[p]
            rest = [a for a in range(3) if a != a0]
            arrive(cps[p])
            q2[s, p] = at(q1.at[s, p], rest.index(a1), pos[a1])[...] + r2[s, p, 0] + r2[s, p, 1] + r2[s, p, 2]
            out.append(send_axis(a2, lambda t, p=p: q2.at[s, p, t], lambda k, p=p: r3.at[s, p, k]))
        return out

    def scatter_end(s, cps):
        out = []
        for p in range(2):
            arrive(cps[p])
            out.append(q2[s, p, pos[RS_ORDER[p][2]]] + r3[s, p, 0] + r3[s, p, 1] + r3[s, p, 2])
        return out

    for p in range(2):
        i_acc[p] = it[0, p, z, y, x].astype(F32)
    arrive(u_first)
    for h in range(2):
        u_acc[h] = ut[0, h].astype(F32)

    item_product(0)
    rs = scatter_start(0)
    for s in range(LAYERS):
        if s > 0:
            arrive(ag)
            ag = gather_start(s, 0)
            arrive(ag)
            ag = gather_start(s, 1)
        rs = scatter_mid(s, rs)
        arrive(ag)
        ux = user_product(s)
        rs = scatter_last(s, rs)
        arrive(ux)
        for h in range(2):
            nxt = (up[s, h] + up_in[s, h]).astype(BF16)
            u_acc[h] += nxt.astype(F32)
            if s + 1 < LAYERS:
                ut[s + 1, h] = nxt
        if s + 1 < LAYERS:
            item_product(s + 1)
            rs_next = scatter_start(s + 1)
        new = scatter_end(s, rs)
        for p in range(2):
            nxt = new[p].astype(BF16)
            i_acc[p] += nxt.astype(F32)
            if s + 1 < LAYERS:
                it[s + 1, p, z, y, x] = nxt
        if s + 1 < LAYERS:
            ag = gather_start(s + 1, 2)
            rs = rs_next

    for p in range(2):
        fin_b[p, x] = (i_acc[p] * 0.25).astype(BF16)
    fb = send_axis(2, lambda t: fin_b.at[:, x], lambda k: fin_b.at[:, x])
    for h in range(2):
        ut[LAYERS, h] = (u_acc[h] * 0.25).astype(BF16)
    own_u = ut[LAYERS, col]
    fu_ref[...] = own_u.astype(F32).T.astype(BF16)

    tiles = n_batch // CHUNK
    iota = lax.broadcasted_iota(jnp.int32, (users, CHUNK), 0)

    def put_rows(group, t, picked):
        for r in range(4):
            rt = 4 * group + r
            for l in range(2):
                lt = 2 * t + l
                sel[lt // 8, (lt % 8) // 4, lt % 4, rt // 3, rt % 3] = picked[16 * r:16 * r + 16, 128 * l:128 * l + 128].astype(BF16)

    base_u = (2 * row + col) * users
    for t in range(tiles):
        ids = ids_ref[0:1, t * CHUNK:(t + 1) * CHUNK]
        hot = jnp.where(iota == ids - base_u, 1.0, 0.0).astype(BF16)
        put_rows(0, t, jnp.dot(own_u, hot, preferred_element_type=F32))
    arrive(fb)
    fin_chunk = join_blocks(lambda part, q: fin_b[part, q])
    nat_f[...] = fin_chunk.astype(F32).T
    own = pl.ds(pl.multiple_of(x * EMB, EMB), EMB)
    fi_ref[...] = nat_f[own, :].astype(BF16)
    base_i = (col * NCHUNK + z * SIDE + y) * CHUNK
    iota_i = lax.broadcasted_iota(jnp.int32, (CHUNK, CHUNK), 0)
    for g in range(1, 3):
        for t in range(tiles):
            rel = ids_ref[g:g + 1, t * CHUNK:(t + 1) * CHUNK] - base_i
            rel = jnp.where((rel >= x * EMB) & (rel < x * EMB + EMB), rel, -1)
            hot = jnp.where(iota_i == rel, 1.0, 0.0).astype(BF16)
            put_rows(g, t, jnp.dot(fin_chunk, hot, preferred_element_type=F32))

    sx = [send(sel.at[1 - col], sel_in, partner)]
    arrive(sx)
    w0[...] = sel[col] + sel_in[...]
    ax0, ax2 = (0, 2), (2, 0)
    cps = [send_axis(ax0[p], lambda t, p=p: w0.at[p, t], lambda k, p=p: in1.at[p, k]) for p in range(2)]
    nxt_cps = []
    for p in range(2):
        arrive(cps[p])
        w1[p] = w0[p, pos[ax0[p]]] + in1[p, 0] + in1[p, 1] + in1[p, 2]
        nxt_cps.append(send_axis(1, lambda t, p=p: w1.at[p, t], lambda k, p=p: in2.at[p, k]))
    cps, nxt_cps = nxt_cps, []
    for p in range(2):
        arrive(cps[p])
        w2[p] = w1[p, y] + in2[p, 0] + in2[p, 1] + in2[p, 2]
        nxt_cps.append(send_axis(ax2[p], lambda t, p=p: w2.at[p], lambda k, p=p: in3.at[p, k]))
    cps, nxt_cps = nxt_cps, []
    for p in range(2):
        arrive(cps[p])
        a = pos[ax0[p]]
        rows_all[col, p, a, y] = w2[p] + in3[p, 0] + in3[p, 1] + in3[p, 2]
        ref = rows_all.at[col, p, a, y]
        nxt_cps.append(send_axis(1, lambda t, ref=ref: ref, lambda k, ref=ref: ref))
    cps, nxt_cps = nxt_cps, []
    for p in range(2):
        arrive(cps[p])
        ref = rows_all.at[col, p, pos[ax0[p]]]
        nxt_cps.append(send_axis(ax0[p], lambda t, ref=ref: ref, lambda k, ref=ref: ref))
    for p in range(2):
        arrive(nxt_cps[p])
    arrive([send(rows_all.at[col], rows_all.at[col], partner)])

    total = jnp.zeros((1, 128), F32)
    for lt in range(n_batch // 128):
        def rows_of(group):
            return jnp.concatenate([rows_all[lt // 8, (lt % 8) // 4, lt % 4, rt // 3, rt % 3].astype(F32)
                                    for rt in range(4 * group, 4 * group + 4)], axis=0)
        e_user, e_pos, e_neg = rows_of(0), rows_of(1), rows_of(2)
        margin = jnp.sum(e_user * e_pos, axis=0, keepdims=True) - jnp.sum(e_user * e_neg, axis=0, keepdims=True)
        soft = jnp.maximum(-margin, 0.0) + jnp.log1p(jnp.exp(-jnp.abs(margin)))
        total = total + soft
        coef = -jax.nn.sigmoid(-margin) / n_batch
        lanes = slice(lt * 128, lt * 128 + 128)
        for ref, g in ((grad_u, coef * (e_pos - e_neg)), (grad_i, coef * e_user)):
            hi = g.astype(BF16)
            left = g - hi.astype(F32)
            mid = left.astype(BF16)
            ref[0:EMB, lanes] = hi
            ref[EMB:2 * EMB, lanes] = mid
            ref[2 * EMB:3 * EMB, lanes] = (left - mid.astype(F32)).astype(BF16)
    loss_ref[...] = jnp.sum(total, axis=1, keepdims=True) / n_batch

    iota2 = lax.broadcasted_iota(jnp.int32, (2 * users, CHUNK), 0)
    prod_i[...] = jnp.zeros_like(prod_i)
    prod_u[...] = jnp.zeros_like(prod_u)
    for t in range(tiles):
        cut = slice(t * CHUNK, (t + 1) * CHUNK)
        plus = jnp.where(iota_i == ids_ref[1:2, cut] - base_i, 1.0, 0.0)
        minus = jnp.where(iota_i == ids_ref[2:3, cut] - base_i, 1.0, 0.0)
        prod_i[...] += lax.dot_general(grad_i[:, cut], (plus - minus).astype(BF16), NT, preferred_element_type=F32)
    seed = (prod_i[0:EMB, :] + prod_i[EMB:2 * EMB, :] + prod_i[2 * EMB:3 * EMB, :]) * 0.25
    s0 = LAYERS
    for part in range(2):
        for q in range(SIDE):
            block = seed[block_rows(part, q), block_lanes(q)]
            s_item[part, q] = block
            it[s0, part, z, y, q] = block.astype(BF16)
    ag = gather_start(s0, 0)
    for t in range(tiles):
        cut = slice(t * CHUNK, (t + 1) * CHUNK)
        hot = jnp.where(iota2 == ids_ref[0:1, cut] - row * (2 * users), 1.0, 0.0).astype(BF16)
        prod_u[...] += lax.dot_general(grad_u[:, cut], hot, NT, preferred_element_type=F32)
    seed = (prod_u[0:EMB, :] + prod_u[EMB:2 * EMB, :] + prod_u[2 * EMB:3 * EMB, :]) * 0.25
    for h in range(2):
        s_user[h] = seed[:, h * users:(h + 1) * users]
        ut[s0, h] = seed[:, h * users:(h + 1) * users].astype(BF16)

    item_product(s0)
    rs = scatter_start(s0)
    for s in range(s0, STAGES):
        arrive(ag)
        if s > s0:
            ag = gather_start(s, 0)
            arrive(ag)
        ag = gather_start(s, 1)
        rs = scatter_mid(s, rs)
        arrive(ag)
        ux = user_product(s)
        rs = scatter_last(s, rs)
        arrive(ux)
        if s + 1 < STAGES:
            for h in range(2):
                ut[s + 1, h] = (s_user[h] + (up[s, h] + up_in[s, h])).astype(BF16)
            item_product(s + 1)
            rs_next = scatter_start(s + 1)
        else:
            gu_ref[...] = (s_user[col] + (up[s, col] + up_in[s, col])).T
        new = scatter_end(s, rs)
        for p in range(2):
            nxt = s_item[p, x] + new[p]
            if s + 1 < STAGES:
                it[s + 1, p, z, y, x] = nxt.astype(BF16)
            else:
                fin_f[p, x] = nxt
        if s + 1 < STAGES:
            ag = gather_start(s + 1, 2)
            rs = rs_next
    ff = send_axis(2, lambda t: fin_f.at[:, x], lambda k: fin_f.at[:, x])
    arrive(ff)
    nat_f[...] = join_blocks(lambda part, q: fin_f[part, q]).T
    gi_ref[...] = nat_f[own, :]
    for cp in sent:
        cp.wait_send()


def solution(mesh):
    def local_fn(mask_blk, user_emb, item_emb, triples):
        n_u, n_b = mask_blk.shape[0], triples.shape[0]
        half = n_u // 2
        vm = pltpu.VMEM
        outs = (jax.ShapeDtypeStruct((half, EMB), BF16), jax.ShapeDtypeStruct((EMB, EMB), BF16),
                jax.ShapeDtypeStruct((1, 1), F32), jax.ShapeDtypeStruct((half, EMB), F32),
                jax.ShapeDtypeStruct((EMB, EMB), F32))
        tile = (16, 128)
        S = SIDE
        scratch = [
            vm((NCHUNK, n_u, CHUNK), jnp.int32), vm((NCHUNK, n_u, CHUNK), BF16),
            vm((n_u, 128), jnp.int32), vm((n_u, 128), jnp.int32), vm((n_u, 128), F32),
            vm((3, 32, 128), jnp.int32), vm((3, 3, 32, 128), jnp.int32), vm((32, 128), F32),
            vm((STAGES, 2, EMB, half), BF16), vm((STAGES, 2, EMB, half), F32), vm((STAGES, 2, EMB, half), F32),
            vm((2, EMB, half), F32), vm((2, EMB, half), F32),
            vm((S, EMB, EMB), BF16), vm((STAGES, 2, S, S, S) + tile, BF16), vm((STAGES, 2, S, S, S) + tile, F32),
            vm((STAGES, 2, S, S) + tile, F32), vm((STAGES, 2, S) + tile, F32),
            vm((STAGES, 2, 3, S, S) + tile, F32), vm((STAGES, 2, 3, S) + tile, F32), vm((STAGES, 2, 3) + tile, F32),
            vm((2,) + tile, F32), vm((2, S) + tile, F32),
            vm((2, S) + tile, BF16), vm((2, S) + tile, F32), vm((CHUNK, EMB), F32),
            vm((2, 2, S, S, 3) + tile, BF16), vm((2, S, S, 3) + tile, BF16), vm((2, S, S, 3) + tile, BF16),
            vm((2, S, 3) + tile, BF16), vm((2, 3) + tile, BF16),
            vm((2, 3, S, 3) + tile, BF16), vm((2, 3, 3) + tile, BF16), vm((2, 3, 3) + tile, BF16),
            vm((2, 2, S, S, 3) + tile, BF16),
            vm((3 * EMB, n_b), BF16), vm((3 * EMB, n_b), BF16),
            vm((3 * EMB, n_u), F32), vm((3 * EMB, CHUNK), F32),
            pltpu.SemaphoreType.DMA((NCHUNK,)), pltpu.SemaphoreType.DMA((NSEM,)), pltpu.SemaphoreType.DMA((NSEM,)),
        ]
        spec = pl.BlockSpec(memory_space=pltpu.VMEM)
        fu, fi, loss, gu, gi = pl.pallas_call(
            kernel,
            out_shape=outs,
            in_specs=[pl.BlockSpec(memory_space=pl.ANY), spec, spec, spec],
            out_specs=(spec,) * 5,
            scratch_shapes=scratch,
            compiler_params=pltpu.CompilerParams(collective_id=0, has_side_effects=True, vmem_limit_bytes=56 * 1024 * 1024),
        )(mask_blk, user_emb, item_emb, triples.T)
        return fu, fi, loss[0, 0], gu, gi

    user_spec = P(('row', 'col'), None)
    item_spec = P(('col', 'row'), None)
    return jax.shard_map(local_fn, mesh=mesh, in_specs=(P('row', 'col'), user_spec, item_spec, P()),
                         out_specs=(user_spec, item_spec, P(), user_spec, item_spec), check_vma=False)
```

time: 3860 us -> 205 us (0.05)
  waiting for transfers between devices: 2280 us -> 0 us
  blocking collectives: 1420 us -> 0 us
  Pallas kernels: 0 us -> 195 us
  other arithmetic: 62.3 us -> 0 us
  matrix products: 52.2 us -> 0 us
    reduce_scatter x12 -> x0, waiting for transfers between devices: 2130 us -> none  [the longest x6 2120 us: item_half(): return lax.psum_scatter(partial_sum, 'row', scatter_dimension=0, tiled=True)]
    all_gather x12 -> x0, blocking collectives: 1070 us -> none  [the longest x6 1060 us: user_half(): gathered = lax.all_gather(item_shard, 'row', axis=0, tiled=True)]
    psum x2 -> x0, blocking collectives: 352 us -> none  [the longest x1 350 us: local_fn(): lax.psum(jnp.sum(mask_blk, axis=0, dtype=jnp.int32), 'row')]
    pallas_call x0 -> x1, Pallas kernels: none -> 195 us  [local_fn(): pl.pallas_call(kernel, out_shape=outs, in_specs=[pl.BlockSpec(memory_spac...]
    psum x1 -> x0, waiting for transfers between devices: 155 us -> none  [local_fn(): lax.psum(jnp.concatenate([rows_user, rows_pos, rows_neg], axis=0), ('row'...]
    dot_general x12 -> x0, matrix products: 52.2 us -> none  [the longest x6 28.9 us: item_half(): lax.dot_general(adj_blk, gathered, (((0,), (0,)), ((), ())), preferred_el...]
  transfers between devices with their start and end apart: 13 -> 0, of which waited for: 9 -> 0; matrix products, arithmetic and copies ran while one was open for 1% -> 0% of each run, Pallas kernels for 0% -> 0%
where the time goes in v1:
time: 205 us
  Pallas kernels  195 us (95%)
  local copies, waits for them, and re-layouts  7.35 us (4%)
  between operations  2.4 us (1%)
    pallas_call x1, Pallas kernels, local_fn(): pl.pallas_call(kernel, out_shape=outs, in_specs=[pl.BlockSpec(memory_spac...  195 us
    unnamed x5, local copies, waits for them, and re-layouts  7.35 us

profile of v1, /device:TPU:0, one launch (start us, length us, event | category | flops | bytes accessed | tf_op | source)
XLA Modules:
  0.0 204.9 jit_solution(13155427515604026569)
XLA Ops:
  0.6 1.5 copy.9.user_ref
  2.1 195.1 %shard_map.83 = (bf16[256,64]{1,0:T(8,128)(2,1)}, bf16[64,64]{1,0:T(8,128)(2,1)}, f32[1,1]{1,0:T(1,128)}, f32[256,64]{1,0:T(8,128)}, f32[64,64]{1,0:T(8,128)}) custom-call(s32[512,4096]{1,0:T(8,128)} %mask_hbm.1, bf16[256,64]{1,0:T(8,128)(2,1)} %copy.9.user_ref, bf16[64,64]{1,0:T(8,128)(2,1)} %item_ref.1, s32[3,2048]{1,0:T(4,128)} %bitcast.2), custom_call_target="tpu_custom_call" | custom-call | tf_op jit(solution)/shard_map/pallas_call | solution.py:419
  197.2 1.5 copy.10
  198.8 1.6 copy.11
  200.4 1.3 copy.15
  202.3 1.4 copy.17

commit v2 on v1

--- a/solution.py
+++ b/solution.py
@@ -12,10 +12,10 @@
 NCHUNK = 16
 LAYERS = 3
 STAGES = 2 * LAYERS
-RS_ORDER = ((0, 1, 2), (2, 1, 0))
 F32 = jnp.float32
 BF16 = jnp.bfloat16
 NSEM = 480
+PLANE_ORDER = (10, 6, 9, 11, 14, 5, 7, 13, 15, 2, 8, 1, 3, 4, 12)
 NT = (((1,), (1,)), ((), ()))
 MESH = pl.DeviceIdType.MESH
 
@@ -40,19 +40,21 @@
            fu_ref, fi_ref, loss_ref, gu_ref, gi_ref,
            mask, adj, rowsum, rowsum_in, scale_u, colsum, colsum_in, scale_i,
            ut, up, up_in, u_acc, s_user,
-           nat, it, part_sum, q1, q2, r1, r2, r3, i_acc, s_item,
+           nat, it, part_sum, q1, r1, r2, i_acc, s_item,
            fin_b, fin_f, nat_f,
            sel, sel_in, w0, w1, w2, in1, in2, in3, rows_all, grad_u, grad_i, prod_u, prod_i,
            mask_sem, send_sem, recv_sem):
     row = lax.axis_index('row')
     col = lax.axis_index('col')
-    pos = (row // 16, (row // 4) % 4, row % 4)
+    pos = (lax.div(row, 16), lax.rem(lax.div(row, 4), 4), lax.rem(row, 4))
+    step = [[p] + [lax.rem(p + k, SIDE) for k in range(1, SIDE)] for p in pos]
+    offset = [[(step[a][k] - pos[a]) * STRIDE[a] if k else 0 for k in range(SIDE)] for a in range(3)]
     z, y, x = pos
-    users = user_ref.shape[0]
+    users = user_ref.shape[1]
     n_batch = ids_ref.shape[1]
 
     def peer(axis, k):
-        return {'row': row + ((pos[axis] + k) % SIDE - pos[axis]) * STRIDE[axis]}
+        return {'row': row + offset[axis][k]}
 
     partner = {'col': 1 - col}
 
@@ -62,12 +64,19 @@
         cp.start()
         copies.append(cp)
 
+    def plane_peer(axes, k):
+        return {'row': row + offset[axes[0]][k // SIDE] + offset[axes[1]][k % SIDE]}
+
     barrier = pltpu.get_barrier_semaphore()
     for axis in range(3):
         for k in range(1, SIDE):
             pl.semaphore_signal(barrier, inc=1, device_id=peer(axis, k), device_id_type=MESH)
+    for axes in ((0, 1), (0, 2), (1, 2)):
+        for k in range(SIDE * SIDE):
+            if k // SIDE and k % SIDE:
+                pl.semaphore_signal(barrier, inc=1, device_id=plane_peer(axes, k), device_id_type=MESH)
     pl.semaphore_signal(barrier, inc=1, device_id=partner, device_id_type=MESH)
-    pl.semaphore_wait(barrier, 10)
+    pl.semaphore_wait(barrier, 37)
 
     sent = []
 
@@ -80,13 +89,17 @@
         return cp
 
     def send_axis(axis, src, dst):
-        return [send(src((pos[axis] + k) % SIDE), dst(k - 1), peer(axis, k)) for k in range(1, SIDE)]
+        return [send(src(step[axis][k]), dst(k - 1), peer(axis, k)) for k in (1, 3, 2)]
+
+    def send_plane(axes, src, dst):
+        return [send(src(step[axes[0]][k // SIDE], step[axes[1]][k % SIDE]), dst(k - 1), plane_peer(axes, k))
+                for k in PLANE_ORDER]
 
     def arrive(cps):
         for cp in cps:
             cp.wait_recv()
 
-    ut[0, col] = user_ref[...].astype(F32).T.astype(BF16)
+    ut[0, col] = user_ref[...]
     u_first = [send(ut.at[0, col], ut.at[0, col], partner)]
     nat[x] = item_ref[...]
     i_first = send_axis(2, lambda t: nat.at[x], lambda k: nat.at[x])
@@ -138,65 +151,68 @@
         adj[j, :, :128] = (su * m[:, :128] * scale_i[2 * j:2 * j + 1, :]).astype(BF16)
         adj[j, :, 128:] = (su * m[:, 128:] * scale_i[2 * j + 1:2 * j + 2, :]).astype(BF16)
 
-    def item_product(s):
+    def at(ref, axis, t):
+        return ref.at[(slice(None),) * axis + (t,)]
+
+    def item_product(s, hold=False):
         lhs = jnp.concatenate([ut[s, 0], ut[s, 1]], axis=1)
-
-        def body(zz, _):
+        first = []
+        for k in (2, 1, 3, 0):
+            zz = step[0][k]
             for yy in range(SIDE):
                 out = jnp.dot(lhs, adj[zz * SIDE + yy], preferred_element_type=F32)
                 for part in range(2):
                     for q in range(SIDE):
                         part_sum[s, part, zz, yy, q] = out[block_rows(part, q), block_lanes(q)]
-            return 0
-
-        lax.fori_loop(0, SIDE, body, 0)
-
-    def user_product(s):
-        def body(zz, acc):
-            for yy in range(SIDE):
-                lhs = join_blocks(lambda part, q: it[s, part, zz, yy, q])
-                acc = acc + lax.dot_general(lhs, adj[zz * SIDE + yy], NT, preferred_element_type=F32)
-            return acc
-
-        acc = lax.fori_loop(0, SIDE, body, jnp.zeros((EMB, 2 * users), F32))
-        up[s, 0] = acc[:, :users]
-        up[s, 1] = acc[:, users:]
-        return [send(up.at[s], up_in.at[s], partner)]
-
-    def at(ref, axis, t):
-        return ref.at[(slice(None),) * axis + (t,)]
-
-    def scatter_start(s):
-        return [send_axis(RS_ORDER[p][0],
-                          lambda t, p=p: at(part_sum.at[s, p], RS_ORDER[p][0], t),
-                          lambda k, p=p: r1.at[s, p, k]) for p in range(2)]
+            if k and not hold:
+                first.append(send(part_sum.at[s, 0, zz], r1.at[s, 0, k - 1], peer(0, k)))
+        return first
+
+    def scatter_start(s, first=None):
+        if not first:
+            first = send_axis(0, lambda t: part_sum.at[s, 0, t], lambda k: r1.at[s, 0, k])
+        return [first, send_axis(2, lambda t: part_sum.at[s, 1, :, :, t], lambda k: r1.at[s, 1, k])]
+
+    REST = ((1, 2), (0, 1))
 
     def scatter_mid(s, cps):
         out = []
         for p in range(2):
-            a0, a1, _ = RS_ORDER[p]
             arrive(cps[p])
-            q1[s, p] = at(part_sum.at[s, p], a0, pos[a0])[...] + r1[s, p, 0] + r1[s, p, 1] + r1[s, p, 2]
-            rest = [a for a in range(3) if a != a0]
-            out.append(send_axis(a1, lambda t, p=p: at(q1.at[s, p], rest.index(a1), t), lambda k, p=p: r2.at[s, p, k]))
-        return out
-
-    def scatter_last(s, cps):
-        out = []
-        for p in range(2):
-            a0, a1, a2 = RS_ORDER[p]
-            rest = [a for a in range(3) if a != a0]
-            arrive(cps[p])
-            q2[s, p] = at(q1.at[s, p], rest.index(a1), pos[a1])[...] + r2[s, p, 0] + r2[s, p, 1] + r2[s, p, 2]
-            out.append(send_axis(a2, lambda t, p=p: q2.at[s, p, t], lambda k, p=p: r3.at[s, p, k]))
+            own = part_sum[s, 0, z] if p == 0 else part_sum[s, 1, :, :, x]
+            q1[s, p] = own + r1[s, p, 0] + r1[s, p, 1] + r1[s, p, 2]
+            out.append(send_plane(REST[p], lambda t0, t1, p=p: q1.at[s, p, t0, t1], lambda k, p=p: r2.at[s, p, k]))
         return out
 
     def scatter_end(s, cps):
         out = []
         for p in range(2):
             arrive(cps[p])
-            out.append(q2[s, p, pos[RS_ORDER[p][2]]] + r3[s, p, 0] + r3[s, p, 1] + r3[s, p, 2])
+            out.append(q1[s, p, pos[REST[p][0]], pos[REST[p][1]]] + jnp.sum(r2[s, p], axis=0))
         return out
+
+    def user_group(s, yy, first):
+        acc = None
+        for zz in range(SIDE):
+            lhs = join_blocks(lambda part, q: it[s, part, zz, yy, q])
+            d = lax.dot_general(lhs, adj[zz * SIDE + yy], NT, preferred_element_type=F32)
+            acc = d if acc is None else acc + d
+        for h in range(2):
+            v = acc[:, h * users:(h + 1) * users]
+            up[s, h] = v if first else up[s, h] + v
+
+    def gather_plane(s):
+        ref = it.at[s, :, z, y, x]
+        return send_plane((0, 2), lambda t0, t1: ref, lambda k: ref)
+
+    def user_own(s):
+        user_group(s, y, True)
+
+    def user_rest(s, ag):
+        for cp, k in zip(ag, (1, 3, 2)):
+            cp.wait_recv()
+            user_group(s, step[1][SIDE - k], False)
+        return [send(up.at[s], up_in.at[s], partner)]
 
     for p in range(2):
         i_acc[p] = it[0, p, z, y, x].astype(F32)
@@ -204,27 +220,31 @@
     for h in range(2):
         u_acc[h] = ut[0, h].astype(F32)
 
-    item_product(0)
-    rs = scatter_start(0)
-    for s in range(LAYERS):
-        if s > 0:
-            arrive(ag)
-            ag = gather_start(s, 0)
-            arrive(ag)
-            ag = gather_start(s, 1)
-        rs = scatter_mid(s, rs)
-        arrive(ag)
-        ux = user_product(s)
-        rs = scatter_last(s, rs)
-        arrive(ux)
+    def user_next(s):
         for h in range(2):
             nxt = (up[s, h] + up_in[s, h]).astype(BF16)
             u_acc[h] += nxt.astype(F32)
             if s + 1 < LAYERS:
                 ut[s + 1, h] = nxt
-        if s + 1 < LAYERS:
-            item_product(s + 1)
-            rs_next = scatter_start(s + 1)
+
+    rs = scatter_start(0, item_product(0))
+    arrive(ag)
+    for k in range(SIDE):
+        user_group(0, step[1][k], k == 0)
+    ux = [send(up.at[0], up_in.at[0], partner)]
+    arrive(ux)
+    user_next(0)
+    item_product(1, hold=True)
+    rs = scatter_mid(0, rs)
+    for s in range(LAYERS):
+        if s == 0:
+            rs_next = scatter_start(1)
+        else:
+            arrive(ag)
+            ag = gather_start(s, 1)
+            user_own(s)
+            rs = scatter_mid(s, rs)
+            ux = user_rest(s, ag)
         new = scatter_end(s, rs)
         for p in range(2):
             nxt = new[p].astype(BF16)
@@ -232,45 +252,50 @@
             if s + 1 < LAYERS:
                 it[s + 1, p, z, y, x] = nxt
         if s + 1 < LAYERS:
-            ag = gather_start(s + 1, 2)
-            rs = rs_next
-
+            ag = gather_plane(s + 1)
+        if s > 0:
+            arrive(ux)
+            user_next(s)
+            if s + 1 < LAYERS:
+                rs_next = scatter_start(s + 1, item_product(s + 1))
+        rs = rs_next
+
+    tiles = n_batch // CHUNK
+    iota = lax.broadcasted_iota(jnp.int32, (users, CHUNK), 0)
     for p in range(2):
         fin_b[p, x] = (i_acc[p] * 0.25).astype(BF16)
     fb = send_axis(2, lambda t: fin_b.at[:, x], lambda k: fin_b.at[:, x])
     for h in range(2):
         ut[LAYERS, h] = (u_acc[h] * 0.25).astype(BF16)
     own_u = ut[LAYERS, col]
-    fu_ref[...] = own_u.astype(F32).T.astype(BF16)
-
-    tiles = n_batch // CHUNK
-    iota = lax.broadcasted_iota(jnp.int32, (users, CHUNK), 0)
-
-    def put_rows(group, t, picked):
-        for r in range(4):
-            rt = 4 * group + r
-            for l in range(2):
-                lt = 2 * t + l
-                sel[lt // 8, (lt % 8) // 4, lt % 4, rt // 3, rt % 3] = picked[16 * r:16 * r + 16, 128 * l:128 * l + 128].astype(BF16)
+    fu_ref[...] = own_u
+
+    def put_rows(rt, t, picked):
+        for l in range(2):
+            lt = 2 * t + l
+            sel[lt // 8, (lt % 8) // 4, lt % 4, rt // 3, rt % 3] = picked[:, 128 * l:128 * l + 128].astype(BF16)
 
     base_u = (2 * row + col) * users
     for t in range(tiles):
         ids = ids_ref[0:1, t * CHUNK:(t + 1) * CHUNK]
         hot = jnp.where(iota == ids - base_u, 1.0, 0.0).astype(BF16)
-        put_rows(0, t, jnp.dot(own_u, hot, preferred_element_type=F32))
-    arrive(fb)
-    fin_chunk = join_blocks(lambda part, q: fin_b[part, q])
-    nat_f[...] = fin_chunk.astype(F32).T
-    own = pl.ds(pl.multiple_of(x * EMB, EMB), EMB)
-    fi_ref[...] = nat_f[own, :].astype(BF16)
+        picked = jnp.dot(own_u, hot, preferred_element_type=F32)
+        for r in range(4):
+            put_rows(r, t, picked[16 * r:16 * r + 16])
     base_i = (col * NCHUNK + z * SIDE + y) * CHUNK
     iota_i = lax.broadcasted_iota(jnp.int32, (CHUNK, CHUNK), 0)
+    iota_b = lax.broadcasted_iota(jnp.int32, (128, CHUNK), 0)
+    x_half, x_side = lax.div(x, 2), lax.rem(x, 2)
+    base_b = base_i + 128 * x_side
+    own_i = jnp.concatenate([fin_b[0, x], fin_b[1, x]], axis=0)
     for g in range(1, 3):
         for t in range(tiles):
-            rel = ids_ref[g:g + 1, t * CHUNK:(t + 1) * CHUNK] - base_i
-            rel = jnp.where((rel >= x * EMB) & (rel < x * EMB + EMB), rel, -1)
-            hot = jnp.where(iota_i == rel, 1.0, 0.0).astype(BF16)
-            put_rows(g, t, jnp.dot(fin_chunk, hot, preferred_element_type=F32))
+            hot = jnp.where(iota_b == ids_ref[g:g + 1, t * CHUNK:(t + 1) * CHUNK] - base_b, 1.0, 0.0).astype(BF16)
+            picked = jnp.dot(own_i, hot, preferred_element_type=F32)
+            for part in range(2):
+                rows = picked[16 * part:16 * part + 16]
+                for half in range(2):
+                    put_rows(4 * g + 2 * part + half, t, jnp.where(x_half == half, rows, 0.0))
 
     sx = [send(sel.at[1 - col], sel_in, partner)]
     arrive(sx)
@@ -278,6 +303,10 @@
     ax0, ax2 = (0, 2), (2, 0)
     cps = [send_axis(ax0[p], lambda t, p=p: w0.at[p, t], lambda k, p=p: in1.at[p, k]) for p in range(2)]
     nxt_cps = []
+    arrive(fb)
+    nat_f[...] = join_blocks(lambda part, q: fin_b[part, q]).astype(F32).T
+    own = pl.ds(pl.multiple_of(x * EMB, EMB), EMB)
+    fi_ref[...] = nat_f[own, :].astype(BF16)
     for p in range(2):
         arrive(cps[p])
         w1[p] = w0[p, pos[ax0[p]]] + in1[p, 0] + in1[p, 1] + in1[p, 2]
@@ -348,26 +377,13 @@
         s_user[h] = seed[:, h * users:(h + 1) * users]
         ut[s0, h] = seed[:, h * users:(h + 1) * users].astype(BF16)
 
-    item_product(s0)
-    rs = scatter_start(s0)
+    rs = scatter_start(s0, item_product(s0))
     for s in range(s0, STAGES):
         arrive(ag)
-        if s > s0:
-            ag = gather_start(s, 0)
-            arrive(ag)
         ag = gather_start(s, 1)
+        user_own(s)
         rs = scatter_mid(s, rs)
-        arrive(ag)
-        ux = user_product(s)
-        rs = scatter_last(s, rs)
-        arrive(ux)
-        if s + 1 < STAGES:
-            for h in range(2):
-                ut[s + 1, h] = (s_user[h] + (up[s, h] + up_in[s, h])).astype(BF16)
-            item_product(s + 1)
-            rs_next = scatter_start(s + 1)
-        else:
-            gu_ref[...] = (s_user[col] + (up[s, col] + up_in[s, col])).T
+        ux = user_rest(s, ag)
         new = scatter_end(s, rs)
         for p in range(2):
             nxt = s_item[p, x] + new[p]
@@ -376,9 +392,16 @@
             else:
                 fin_f[p, x] = nxt
         if s + 1 < STAGES:
-            ag = gather_start(s + 1, 2)
-            rs = rs_next
-    ff = send_axis(2, lambda t: fin_f.at[:, x], lambda k: fin_f.at[:, x])
+            ag = gather_plane(s + 1)
+        else:
+            ff = send_axis(2, lambda t: fin_f.at[:, x], lambda k: fin_f.at[:, x])
+        arrive(ux)
+        if s + 1 < STAGES:
+            for h in range(2):
+                ut[s + 1, h] = (s_user[h] + (up[s, h] + up_in[s, h])).astype(BF16)
+            rs = scatter_start(s + 1, item_product(s + 1))
+        else:
+            gu_ref[...] = s_user[col] + (up[s, col] + up_in[s, col])
     arrive(ff)
     nat_f[...] = join_blocks(lambda part, q: fin_f[part, q]).T
     gi_ref[...] = nat_f[own, :]
@@ -391,8 +414,8 @@
         n_u, n_b = mask_blk.shape[0], triples.shape[0]
         half = n_u // 2
         vm = pltpu.VMEM
-        outs = (jax.ShapeDtypeStruct((half, EMB), BF16), jax.ShapeDtypeStruct((EMB, EMB), BF16),
-                jax.ShapeDtypeStruct((1, 1), F32), jax.ShapeDtypeStruct((half, EMB), F32),
+        outs = (jax.ShapeDtypeStruct((EMB, half), BF16), jax.ShapeDtypeStruct((EMB, EMB), BF16),
+                jax.ShapeDtypeStruct((1, 1), F32), jax.ShapeDtypeStruct((EMB, half), F32),
                 jax.ShapeDtypeStruct((EMB, EMB), F32))
         tile = (16, 128)
         S = SIDE
@@ -403,8 +426,8 @@
             vm((STAGES, 2, EMB, half), BF16), vm((STAGES, 2, EMB, half), F32), vm((STAGES, 2, EMB, half), F32),
             vm((2, EMB, half), F32), vm((2, EMB, half), F32),
             vm((S, EMB, EMB), BF16), vm((STAGES, 2, S, S, S) + tile, BF16), vm((STAGES, 2, S, S, S) + tile, F32),
-            vm((STAGES, 2, S, S) + tile, F32), vm((STAGES, 2, S) + tile, F32),
-            vm((STAGES, 2, 3, S, S) + tile, F32), vm((STAGES, 2, 3, S) + tile, F32), vm((STAGES, 2, 3) + tile, F32),
+            vm((STAGES, 2, S, S) + tile, F32),
+            vm((STAGES, 2, 3, S, S) + tile, F32), vm((STAGES, 2, S * S - 1) + tile, F32),
             vm((2,) + tile, F32), vm((2, S) + tile, F32),
             vm((2, S) + tile, BF16), vm((2, S) + tile, F32), vm((CHUNK, EMB), F32),
             vm((2, 2, S, S, 3) + tile, BF16), vm((2, S, S, 3) + tile, BF16), vm((2, S, S, 3) + tile, BF16),
@@ -423,8 +446,8 @@
             out_specs=(spec,) * 5,
             scratch_shapes=scratch,
             compiler_params=pltpu.CompilerParams(collective_id=0, has_side_effects=True, vmem_limit_bytes=56 * 1024 * 1024),
-        )(mask_blk, user_emb, item_emb, triples.T)
-        return fu, fi, loss[0, 0], gu, gi
+        )(mask_blk, user_emb.T, item_emb, triples.T)
+        return fu.T, fi, loss[0, 0], gu.T, gi
 
     user_spec = P(('row', 'col'), None)
     item_spec = P(('col', 'row'), None)

time: 205 us -> 158 us (0.77)
  Pallas kernels: 195 us -> 150 us
    pallas_call x1, Pallas kernels: 195 us -> 150 us  [local_fn(): pl.pallas_call(kernel, out_shape=outs, in_specs=[pl.BlockSpec(memory_spac...]
    unnamed x5 -> x4, local copies, waits for them, and re-layouts: 7.35 us -> 5.55 us
where the time goes in v2:
time: 158 us
  Pallas kernels  150 us (95%)
  local copies, waits for them, and re-layouts  5.55 us (4%)
  between operations  2.4 us (2%)
    pallas_call x1, Pallas kernels, local_fn(): pl.pallas_call(kernel, out_shape=outs, in_specs=[pl.BlockSpec(memory_spac...  150 us
    unnamed x4, local copies, waits for them, and re-layouts  5.55 us

profile of v2, /device:TPU:0, one launch (start us, length us, event | category | flops | bytes accessed | tf_op | source)
XLA Modules:
  0.0 158.0 jit_solution(6666665429531580438)
XLA Ops:
  0.6 150.1 %shard_map.83 = (bf16[64,256]{1,0:T(8,128)(2,1)}, bf16[64,64]{1,0:T(8,128)(2,1)}, f32[1,1]{1,0:T(1,128)}, f32[64,256]{1,0:T(8,128)}, f32[64,64]{1,0:T(8,128)}) custom-call(s32[512,4096]{1,0:T(8,128)} %mask_hbm.1, bf16[64,256]{1,0:T(8,128)(2,1)} %bitcast.6, bf16[64,64]{1,0:T(8,128)(2,1)} %item_ref.1, s32[3,2048]{1,0:T(4,128)} %bitcast.7), custom_call_target="tpu_custom_call" | custom-call | tf_op jit(solution)/shard_map/pallas_call | solution.py:442
  150.7 1.4 copy.14
  152.1 1.3 copy.15
  154.0 1.5 copy.17
  155.5 1.4 copy.18

commit v3 on v2

v3 whole, which is shorter than its diff:
```python
import jax
import jax.numpy as jnp
from jax import lax
from jax.experimental import pallas as pl
from jax.experimental.pallas import tpu as pltpu
from jax.sharding import PartitionSpec as P

SIDE = 4
STRIDE = (16, 4, 1)
EMB = 64
CHUNK = 256
NCHUNK = 16
LAYERS = 3
STAGES = 2 * LAYERS
F32 = jnp.float32
BF16 = jnp.bfloat16
NSEM = 160
PLANE_ORDER = (10, 6, 9, 11, 14, 5, 7, 13, 15, 2, 8, 1, 3, 4, 12)
NT = (((1,), (1,)), ((), ()))
MESH = pl.DeviceIdType.MESH


def block_rows(part, q):
    return slice(32 * part + 16 * (q // 2), 32 * part + 16 * (q // 2) + 16)


def block_lanes(q):
    return slice(128 * (q % 2), 128 * (q % 2) + 128)


def join_blocks(get):
    rows = []
    for part in range(2):
        for half in range(2):
            rows.append(jnp.concatenate([get(part, 2 * half), get(part, 2 * half + 1)], axis=1))
    return jnp.concatenate(rows, axis=0)


def kernel(mask_hbm, user_ref, item_ref, ids_ref,
           fu_ref, fi_ref, loss_ref, gu_ref, gi_ref,
           mask, adj, rowsum, rowsum_in, scale_u, colsum, colsum_in, scale_i,
           ut, up, up_in, u_acc, s_user,
           nat, it, part_sum, q1, r1, r2, i_acc, s_item,
           fin_b, fin_f, nat_f,
           sel, sel_in, w0, w1, in1, in2, rows_all, grad_u, grad_i, prod_u, prod_i,
           mask_sem, send_sem, recv_sem):
    row = lax.axis_index('row')
    col = lax.axis_index('col')
    pos = (lax.div(row, 16), lax.rem(lax.div(row, 4), 4), lax.rem(row, 4))
    step = [[p] + [lax.rem(p + k, SIDE) for k in range(1, SIDE)] for p in pos]
    offset = [[(step[a][k] - pos[a]) * STRIDE[a] if k else 0 for k in range(SIDE)] for a in range(3)]
    z, y, x = pos
    users = user_ref.shape[1]
    n_batch = ids_ref.shape[1]

    def peer(axis, k):
        return {'row': row + offset[axis][k]}

    partner = {'col': 1 - col}

    copies = []
    for j in range(NCHUNK):
        cp = pltpu.make_async_copy(mask_hbm.at[:, pl.ds(j * CHUNK, CHUNK)], mask.at[j], mask_sem.at[j])
        cp.start()
        copies.append(cp)

    def plane_peer(axes, k):
        return {'row': row + offset[axes[0]][k // SIDE] + offset[axes[1]][k % SIDE]}

    barrier = pltpu.get_barrier_semaphore()
    for axis in range(3):
        for k in range(1, SIDE):
            pl.semaphore_signal(barrier, inc=1, device_id=peer(axis, k), device_id_type=MESH)
    for axes in ((0, 1), (0, 2), (1, 2)):
        for k in range(SIDE * SIDE):
            if k // SIDE and k % SIDE:
                pl.semaphore_signal(barrier, inc=1, device_id=plane_peer(axes, k), device_id_type=MESH)
    pl.semaphore_signal(barrier, inc=1, device_id=partner, device_id_type=MESH)
    pl.semaphore_wait(barrier, 37)

    count = [0, 0]
    leaving = []

    def fresh(n=1):
        out = (count[0], count[1])
        count[0] += 1
        count[1] += n
        return out

    def send(src, dst, device, sems):
        pltpu.make_async_remote_copy(src_ref=src, dst_ref=dst, send_sem=send_sem.at[sems[0]], recv_sem=recv_sem.at[sems[1]],
                                     device_id=device, device_id_type=MESH).start()

    def left(ref, sems):
        leaving.append((ref, sems[0]))

    def arrive(ref, sems):
        pltpu.make_async_copy(ref, ref, recv_sem.at[sems[1]]).wait()

    def plus(sems, n):
        return (sems[0], sems[1] + n)

    def send_axis(axis, src, dst, sems):
        for k in (1, 3, 2):
            send(src(step[axis][k]), dst(k - 1), peer(axis, k), sems)

    def send_plane(axes, src, dst, sems):
        for k in PLANE_ORDER:
            send(src(step[axes[0]][k // SIDE], step[axes[1]][k % SIDE]), dst(k - 1), plane_peer(axes, k), sems)

    ut[0, col] = user_ref[...]
    u_sem = fresh()
    send(ut.at[0, col], ut.at[0, col], partner, u_sem)
    left(ut.at[0, 0], u_sem)
    nat[x] = item_ref[...]
    n_sem = fresh()
    send_axis(2, lambda t: nat.at[x], lambda k: nat.at[x], n_sem)
    left(nat.at[0:3], n_sem)

    rowsum[...] = jnp.zeros_like(rowsum)
    for j in range(NCHUNK):
        copies[j].wait()
        m = mask[j]
        rowsum[...] += m[:, :128] + m[:, 128:]
        s = jnp.sum(m, axis=0, keepdims=True)
        colsum[0, 2 * j:2 * j + 1, :] = s[:, :128]
        colsum[0, 2 * j + 1:2 * j + 2, :] = s[:, 128:]
    r_sem, c_sem = fresh(), fresh()
    send(rowsum, rowsum_in, partner, r_sem)
    left(rowsum, r_sem)
    send_axis(0, lambda t: colsum.at[0], lambda k: colsum_in.at[k], c_sem)
    left(colsum_in.at[0:3], c_sem)

    arrive(nat.at[0:3], n_sem)
    chunk0 = jnp.concatenate([nat[k].astype(F32) for k in range(SIDE)], axis=0).T
    for part in range(2):
        for q in range(SIDE):
            it[0, part, z, y, q] = chunk0[block_rows(part, q), block_lanes(q)].astype(BF16)

    stage_sem = [dict(user=fresh(), plane=fresh(SIDE), line=fresh(SIDE), axis=[fresh(SIDE), fresh(SIDE)],
                      last=[fresh(), fresh()]) for _ in range(STAGES)]

    def gather_plane(s):
        sems = stage_sem[s]['plane']
        ref = it.at[s, :, z, y, x]
        for k in PLANE_ORDER:
            send(ref, ref, plane_peer((0, 2), k), plus(sems, k // SIDE))
        left(r2.at[s, 0], sems)

    def gather_line(s):
        sems = stage_sem[s]['plane']
        ref = it.at[s, :, z, y]
        for k in (1, 3, 2):
            send(ref, ref, peer(0, k), plus(sems, k))
        left(it.at[s, :, 0:3, 0], sems)

    def gather_last(s, line=False):
        sems = stage_sem[s]
        for kz in (0, 1, 3, 2):
            ref = it.at[s, :, step[0][(SIDE - kz) % SIDE], y]
            if kz:
                arrive(ref, plus(sems['plane'], kz))
            elif not line:
                arrive(ref.at[:, 0:3], sems['plane'])
            for k in (1, 3, 2):
                send(ref, ref, peer(1, k), plus(sems['line'], k))
        left(r1.at[s, 0], sems['line'])

    gather_line(0)
    arrive(rowsum_in, r_sem)
    deg_u = jnp.maximum(jnp.sum(rowsum[...] + rowsum_in[...], axis=1, keepdims=True), 1)
    scale_u[...] = jnp.broadcast_to(lax.rsqrt(deg_u.astype(F32)), scale_u.shape)
    arrive(colsum_in.at[0:3], c_sem)
    colsum[1] = colsum[0] + colsum_in[0] + colsum_in[1] + colsum_in[2]
    d_sem = fresh()
    send_plane((1, 2), lambda t0, t1: colsum.at[1], lambda k: colsum_in.at[3 + k], d_sem)
    left(colsum_in.at[3:18], d_sem)
    gather_last(0, line=True)
    arrive(colsum_in.at[3:18], d_sem)
    deg_i = jnp.maximum(colsum[1] + jnp.sum(colsum_in[3:], axis=0), 1)
    scale_i[...] = lax.rsqrt(deg_i.astype(F32))
    for j in range(NCHUNK):
        su = scale_u[...]
        m = mask[j].astype(F32)
        adj[j, :, :128] = (su * m[:, :128] * scale_i[2 * j:2 * j + 1, :]).astype(BF16)
        adj[j, :, 128:] = (su * m[:, 128:] * scale_i[2 * j + 1:2 * j + 2, :]).astype(BF16)

    def at(ref, axis, t):
        return ref.at[(slice(None),) * axis + (t,)]

    def item_product(s, hold=False):
        lhs = jnp.concatenate([ut[s, 0], ut[s, 1]], axis=1)

        def body(i, _):
            ky = lax.rem(i + 1, SIDE)
            yy = lax.rem(y + ky, SIDE)
            for kz in (2, 1, 3, 0):
                zz = step[0][kz]
                out = jnp.dot(lhs, adj[zz * SIDE + yy], preferred_element_type=F32)
                for part in range(2):
                    for q in range(SIDE):
                        part_sum[s, part, zz, yy, q] = out[block_rows(part, q), block_lanes(q)]
            if not hold:
                scatter_send(s, ky, yy)
            return 0

        lax.fori_loop(0, SIDE, body, 0)
        for p in range(2):
            left(r1.at[s, p], stage_sem[s]['axis'][p])

    def scatter_send(s, ky, yy):
        sems = stage_sem[s]['axis']
        send_axis(0, lambda t: part_sum.at[s, 0, t, yy], lambda k: r1.at[s, 0, ky, k], plus(sems[0], ky))
        send_axis(2, lambda t: part_sum.at[s, 1, :, yy, t], lambda k: r1.at[s, 1, ky, k], plus(sems[1], ky))

    def scatter_mid(s):
        sems = stage_sem[s]

        def piece(ky, yy, off, ks):
            for p in range(2):
                axis = (2, 0)[p]
                arrive(r1.at[s, p, ky], plus(sems['axis'][p], ky))
                own = part_sum[s, 0, z, yy] if p == 0 else part_sum[s, 1, :, yy, x]
                q1[s, p, ky] = own + jnp.sum(r1[s, p, ky], axis=0)
                for k in ks:
                    send(q1.at[s, p, ky, step[axis][k]], r2.at[s, p, 4 * ky + k - 1], {'row': row + off + offset[axis][k]},
                         sems['last'][p])

        def body(ky, _):
            yy = lax.rem(y + ky, SIDE)
            piece(ky, yy, (yy - y) * STRIDE[1], (2, 1, 3, 0))
            return 0

        lax.fori_loop(1, SIDE, body, 0)
        piece(0, y, 0, (2, 1, 3))
        for p in range(2):
            left(r2.at[s, p], sems['last'][p])

    def scatter_end(s):
        out = []
        for p in range(2):
            arrive(r2.at[s, p], stage_sem[s]['last'][p])
            out.append(q1[s, p, 0, pos[(2, 0)[p]]] + jnp.sum(r2[s, p], axis=0))
        return out

    def user_group(s, yy, first):
        acc = None
        for zz in range(SIDE):
            lhs = join_blocks(lambda part, q: it[s, part, zz, yy, q])
            d = lax.dot_general(lhs, adj[zz * SIDE + yy], NT, preferred_element_type=F32)
            acc = d if acc is None else acc + d
        for h in range(2):
            v = acc[:, h * users:(h + 1) * users]
            up[s, h] = v if first else up[s, h] + v

    def user_own(s):
        user_group(s, y, True)

    def user_rest(s):
        def body(k, _):
            yy = lax.rem(y + SIDE - k, SIDE)
            arrive(it.at[s, :, :, yy], plus(stage_sem[s]['line'], k))
            user_group(s, yy, False)
            return 0

        lax.fori_loop(1, SIDE, body, 0)
        sems = stage_sem[s]['user']
        send(up.at[s], up_in.at[s], partner, sems)
        left(up.at[s], sems)

    def user_there(s):
        arrive(up_in.at[s], stage_sem[s]['user'])

    for p in range(2):
        i_acc[p] = it[0, p, z, y, x].astype(F32)
    arrive(ut.at[0, 1 - col], u_sem)
    for h in range(2):
        u_acc[h] = ut[0, h].astype(F32)

    def user_next(s):
        for h in range(2):
            nxt = (up[s, h] + up_in[s, h]).astype(BF16)
            u_acc[h] += nxt.astype(F32)
            if s + 1 < LAYERS:
                ut[s + 1, h] = nxt

    item_product(0)
    user_own(0)
    user_rest(0)
    user_there(0)
    user_next(0)
    item_product(1, hold=True)
    scatter_mid(0)
    for s in range(LAYERS):
        if s == 0:
            def late(i, _):
                ky = lax.rem(i + 1, SIDE)
                scatter_send(1, ky, lax.rem(y + ky, SIDE))
                return 0
            lax.fori_loop(0, SIDE, late, 0)
        else:
            gather_last(s)
            user_own(s)
            scatter_mid(s)
            user_rest(s)
        new = scatter_end(s)
        for p in range(2):
            nxt = new[p].astype(BF16)
            i_acc[p] += nxt.astype(F32)
            if s + 1 < LAYERS:
                it[s + 1, p, z, y, x] = nxt
        if s + 1 < LAYERS:
            gather_plane(s + 1)
        if s > 0:
            user_there(s)
            user_next(s)
            if s + 1 < LAYERS:
                item_product(s + 1)

    tiles = n_batch // CHUNK
    iota = lax.broadcasted_iota(jnp.int32, (users, CHUNK), 0)
    for p in range(2):
        fin_b[p, x] = (i_acc[p] * 0.25).astype(BF16)
    f_sem = fresh()
    send_axis(2, lambda t: fin_b.at[:, x], lambda k: fin_b.at[:, x], f_sem)
    left(fin_b.at[:, 0:3], f_sem)
    for h in range(2):
        ut[LAYERS, h] = (u_acc[h] * 0.25).astype(BF16)
    own_u = ut[LAYERS, col]
    fu_ref[...] = own_u

    def put_rows(rt, t, picked):
        for l in range(2):
            lt = 2 * t + l
            sel[lt // 8, (lt % 8) // 4, lt % 4, rt // 3, rt % 3] = picked[:, 128 * l:128 * l + 128].astype(BF16)

    base_u = (2 * row + col) * users
    for t in range(tiles):
        ids = ids_ref[0:1, t * CHUNK:(t + 1) * CHUNK]
        hot = jnp.where(iota == ids - base_u, 1.0, 0.0).astype(BF16)
        picked = jnp.dot(own_u, hot, preferred_element_type=F32)
        for r in range(4):
            put_rows(r, t, picked[16 * r:16 * r + 16])
    base_i = (col * NCHUNK + z * SIDE + y) * CHUNK
    iota_i = lax.broadcasted_iota(jnp.int32, (CHUNK, CHUNK), 0)
    iota_b = lax.broadcasted_iota(jnp.int32, (128, CHUNK), 0)
    x_half, x_side = lax.div(x, 2), lax.rem(x, 2)
    base_b = base_i + 128 * x_side
    own_i = jnp.concatenate([fin_b[0, x], fin_b[1, x]], axis=0)
    for g in range(1, 3):
        for t in range(tiles):
            hot = jnp.where(iota_b == ids_ref[g:g + 1, t * CHUNK:(t + 1) * CHUNK] - base_b, 1.0, 0.0).astype(BF16)
            picked = jnp.dot(own_i, hot, preferred_element_type=F32)
            for part in range(2):
                rows = picked[16 * part:16 * part + 16]
                for half in range(2):
                    put_rows(4 * g + 2 * part + half, t, jnp.where(x_half == half, rows, 0.0))

    x_sem = fresh()
    send(sel.at[1 - col], sel_in, partner, x_sem)
    left(sel_in, x_sem)
    arrive(sel_in, x_sem)
    w0[...] = sel[col] + sel_in[...]
    ax0, ax2 = (0, 2), (2, 0)
    sems = [fresh() for _ in range(2)]
    for p in range(2):
        send_plane((ax0[p], 1), lambda t0, t1: w0.at[p, t0, t1], lambda k: in1.at[p, k], sems[p])
        left(in1.at[p], sems[p])
    arrive(fin_b.at[:, 0:3], f_sem)
    nat_f[...] = join_blocks(lambda part, q: fin_b[part, q]).astype(F32).T
    own = pl.ds(pl.multiple_of(x * EMB, EMB), EMB)
    fi_ref[...] = nat_f[own, :].astype(BF16)
    sems2 = [fresh() for _ in range(2)]
    for p in range(2):
        arrive(in1.at[p], sems[p])
        w1[p] = (w0[p, pos[ax0[p]], y].astype(F32) + jnp.sum(in1[p].astype(F32), axis=0)).astype(BF16)
        send_axis(ax2[p], lambda t: w1.at[p], lambda k: in2.at[p, k], sems2[p])
        left(in2.at[p], sems2[p])
    sems3 = [fresh() for _ in range(2)]
    for p in range(2):
        arrive(in2.at[p], sems2[p])
        a = pos[ax0[p]]
        rows_all[col, p, a, y] = w1[p] + in2[p, 0] + in2[p, 1] + in2[p, 2]
        ref = rows_all.at[col, p, a, y]
        send_plane((ax0[p], 1), lambda t0, t1: ref, lambda k: ref, sems3[p])
        left(in1.at[p], sems3[p])
    for p in range(2):
        arrive(in1.at[p], sems3[p])
    o_sem = fresh()
    send(rows_all.at[col], rows_all.at[col], partner, o_sem)
    left(rows_all.at[0], o_sem)
    arrive(rows_all.at[1 - col], o_sem)

    total = jnp.zeros((1, 128), F32)
    for lt in range(n_batch // 128):
        def rows_of(group):
            return jnp.concatenate([rows_all[lt // 8, (lt % 8) // 4, lt % 4, rt // 3, rt % 3].astype(F32)
                                    for rt in range(4 * group, 4 * group + 4)], axis=0)
        e_user, e_pos, e_neg = rows_of(0), rows_of(1), rows_of(2)
        margin = jnp.sum(e_user * e_pos, axis=0, keepdims=True) - jnp.sum(e_user * e_neg, axis=0, keepdims=True)
        soft = jnp.maximum(-margin, 0.0) + jnp.log1p(jnp.exp(-jnp.abs(margin)))
        total = total + soft
        coef = -jax.nn.sigmoid(-margin) / n_batch
        lanes = slice(lt * 128, lt * 128 + 128)
        for ref, g in ((grad_u, coef * (e_pos - e_neg)), (grad_i, coef * e_user)):
            hi = g.astype(BF16)
            low = g - hi.astype(F32)
            mid = low.astype(BF16)
            ref[0:EMB, lanes] = hi
            ref[EMB:2 * EMB, lanes] = mid
            ref[2 * EMB:3 * EMB, lanes] = (low - mid.astype(F32)).astype(BF16)
    loss_ref[...] = jnp.sum(total, axis=1, keepdims=True) / n_batch

    iota2 = lax.broadcasted_iota(jnp.int32, (2 * users, CHUNK), 0)
    prod_i[...] = jnp.zeros_like(prod_i)
    prod_u[...] = jnp.zeros_like(prod_u)
    for t in range(tiles):
        cut = slice(t * CHUNK, (t + 1) * CHUNK)
        pos_hot = jnp.where(iota_i == ids_ref[1:2, cut] - base_i, 1.0, 0.0)
        neg_hot = jnp.where(iota_i == ids_ref[2:3, cut] - base_i, 1.0, 0.0)
        prod_i[...] += lax.dot_general(grad_i[:, cut], (pos_hot - neg_hot).astype(BF16), NT, preferred_element_type=F32)
    seed = (prod_i[0:EMB, :] + prod_i[EMB:2 * EMB, :] + prod_i[2 * EMB:3 * EMB, :]) * 0.25
    s0 = LAYERS
    for part in range(2):
        for q in range(SIDE):
            block = seed[block_rows(part, q), block_lanes(q)]
            s_item[part, q] = block
            it[s0, part, z, y, q] = block.astype(BF16)
    gather_line(s0)
    for t in range(tiles):
        cut = slice(t * CHUNK, (t + 1) * CHUNK)
        hot = jnp.where(iota2 == ids_ref[0:1, cut] - row * (2 * users), 1.0, 0.0).astype(BF16)
        prod_u[...] += lax.dot_general(grad_u[:, cut], hot, NT, preferred_element_type=F32)
    seed = (prod_u[0:EMB, :] + prod_u[EMB:2 * EMB, :] + prod_u[2 * EMB:3 * EMB, :]) * 0.25
    for h in range(2):
        s_user[h] = seed[:, h * users:(h + 1) * users]
        ut[s0, h] = seed[:, h * users:(h + 1) * users].astype(BF16)

    item_product(s0)
    for s in range(s0, STAGES):
        gather_last(s, line=s == s0)
        user_own(s)
        scatter_mid(s)
        user_rest(s)
        new = scatter_end(s)
        for p in range(2):
            nxt = s_item[p, x] + new[p]
            if s + 1 < STAGES:
                it[s + 1, p, z, y, x] = nxt.astype(BF16)
            else:
                fin_f[p, x] = nxt
        if s + 1 < STAGES:
            gather_plane(s + 1)
        else:
            e_sem = fresh()
            send_axis(2, lambda t: fin_f.at[:, x], lambda k: fin_f.at[:, x], e_sem)
            left(fin_f.at[:, 0:3], e_sem)
        user_there(s)
        if s + 1 < STAGES:
            for h in range(2):
                ut[s + 1, h] = (s_user[h] + (up[s, h] + up_in[s, h])).astype(BF16)
            item_product(s + 1)
        else:
            gu_ref[...] = s_user[col] + (up[s, col] + up_in[s, col])
    arrive(fin_f.at[:, 0:3], e_sem)
    nat_f[...] = join_blocks(lambda part, q: fin_f[part, q]).T
    gi_ref[...] = nat_f[own, :]
    for ref, i in leaving:
        pltpu.make_async_copy(ref, ref, send_sem.at[i]).wait()


def hand_over(*refs):
    for src, dst in zip(refs[:5], refs[5:]):
        dst[...] = src[...]


def solution(mesh):
    def local_fn(mask_blk, user_emb, item_emb, triples):
        n_u, n_b = mask_blk.shape[0], triples.shape[0]
        half = n_u // 2
        vm = pltpu.VMEM
        outs = (jax.ShapeDtypeStruct((EMB, half), BF16), jax.ShapeDtypeStruct((EMB, EMB), BF16),
                jax.ShapeDtypeStruct((1, 1), F32), jax.ShapeDtypeStruct((EMB, half), F32),
                jax.ShapeDtypeStruct((EMB, EMB), F32))
        tile = (16, 128)
        S = SIDE
        scratch = [
            vm((NCHUNK, n_u, CHUNK), jnp.int32), vm((NCHUNK, n_u, CHUNK), BF16),
            vm((n_u, 128), jnp.int32), vm((n_u, 128), jnp.int32), vm((n_u, 128), F32),
            vm((2, 32, 128), jnp.int32), vm((18, 32, 128), jnp.int32), vm((32, 128), F32),
            vm((STAGES, 2, EMB, half), BF16), vm((STAGES, 2, EMB, half), F32), vm((STAGES, 2, EMB, half), F32),
            vm((2, EMB, half), F32), vm((2, EMB, half), F32),
            vm((S, EMB, EMB), BF16), vm((STAGES, 2, S, S, S) + tile, BF16), vm((STAGES, 2, S, S, S) + tile, F32),
            vm((STAGES, 2, S, S) + tile, F32),
            vm((STAGES, 2, S, 3, S) + tile, F32), vm((STAGES, 2, S * S - 1) + tile, F32),
            vm((2,) + tile, F32), vm((2, S) + tile, F32),
            vm((2, S) + tile, BF16), vm((2, S) + tile, F32), vm((CHUNK, EMB), F32),
            vm((2, 2, S, S, 3) + tile, BF16), vm((2, S, S, 3) + tile, BF16), vm((2, S, S, 3) + tile, BF16),
            vm((2, 3) + tile, BF16), vm((2, S * S - 1, 3) + tile, BF16), vm((2, 3, 3) + tile, BF16),
            vm((2, 2, S, S, 3) + tile, BF16),
            vm((3 * EMB, n_b), BF16), vm((3 * EMB, n_b), BF16),
            vm((3 * EMB, n_u), F32), vm((3 * EMB, CHUNK), F32),
            pltpu.SemaphoreType.DMA((NCHUNK,)), pltpu.SemaphoreType.DMA((NSEM,)), pltpu.SemaphoreType.DMA((NSEM,)),
        ]
        spec = pl.BlockSpec(memory_space=pltpu.VMEM)
        fu, fi, loss, gu, gi = pl.pallas_call(
            kernel,
            out_shape=outs,
            in_specs=[pl.BlockSpec(memory_space=pl.ANY), spec, spec, spec],
            out_specs=(spec,) * 5,
            scratch_shapes=scratch,
            compiler_params=pltpu.CompilerParams(collective_id=0, has_side_effects=True, vmem_limit_bytes=56 * 1024 * 1024),
        )(mask_blk, user_emb.T, item_emb, triples.T)
        args = (fu, fi, loss, gu, gi)
        fu, fi, loss, gu, gi = pl.pallas_call(hand_over, out_shape=outs, in_specs=[spec] * 5, out_specs=(spec,) * 5)(*args)
        return fu.T, fi, loss[0, 0], gu.T, gi

    user_spec = P(('row', 'col'), None)
    item_spec = P(('col', 'row'), None)
    return jax.shard_map(local_fn, mesh=mesh, in_specs=(P('row', 'col'), user_spec, item_spec, P()),
                         out_specs=(user_spec, item_spec, P(), user_spec, item_spec), check_vma=False)
```

time: 158 us -> 140 us (0.89)
  Pallas kernels: 150 us -> 139 us
  local copies, waits for them, and re-layouts: 5.55 us -> 0 us
  between operations: 2.4 us -> 0.64 us
    pallas_call x1, Pallas kernels: 150 us -> 137 us  [local_fn(): pl.pallas_call(kernel, out_shape=outs, in_specs=[pl.BlockSpec(memory_spac...]
    unnamed x4 -> x0, local copies, waits for them, and re-layouts: 5.55 us -> none
    pallas_call x0 -> x1, Pallas kernels: none -> 2.17 us  [local_fn(): pl.pallas_call(hand_over, out_shape=outs, in_specs=[spec] * 5, out_specs=...]
where the time goes in v3:
time: 140 us; the launch traced here: 139 us
  Pallas kernels  139 us (99%)
    pallas_call x1, Pallas kernels, local_fn(): pl.pallas_call(kernel, out_shape=outs, in_specs=[pl.BlockSpec(memory_spac...  137 us

profile of v3, /device:TPU:0, one launch (start us, length us, event | category | flops | bytes accessed | tf_op | source)
XLA Modules:
  0.0 139.5 jit_solution(7538019294592124988)
XLA Ops:
  0.6 136.7 %shard_map.83 = (bf16[64,256]{1,0:T(8,128)(2,1)}, bf16[64,64]{1,0:T(8,128)(2,1)}, f32[1,1]{1,0:T(1,128)}, f32[64,256]{1,0:T(8,128)}, f32[64,64]{1,0:T(8,128)}) custom-call(s32[512,4096]{1,0:T(8,128)} %mask_hbm.1, bf16[64,256]{1,0:T(8,128)(2,1)} %bitcast.5, bf16[64,64]{1,0:T(8,128)(2,1)} %item_ref.1, s32[3,2048]{1,0:T(4,128)} %bitcast.6), custom_call_target="tpu_custom_call" | custom-call | tf_op jit(solution)/shard_map/pallas_call | solution.py:506
  137.3 2.2 %shard_map.84 = (bf16[64,256]{1,0:T(8,128)(2,1)}, bf16[64,64]{1,0:T(8,128)(2,1)}, f32[1,1]{1,0:T(1,128)}, f32[64,256]{1,0:T(8,128)}, f32[64,64]{1,0:T(8,128)}) custom-call(bf16[64,256]{1,0:T(8,128)(2,1)} %get-tuple-element.15.refs_0_, bf16[64,64]{1,0:T(8,128)(2,1)} %get-tuple-element.16.refs_1_, f32[1,1]{1,0:T(1,128)} %get-tuple-element.17.refs_2_, ...), custom_call_target="tpu_custom_call" | custom-call | tf_op jit(solution)/shard_map/pallas_call | solution.py:515

commit v4 on v3

--- a/solution.py
+++ b/solution.py
@@ -15,6 +15,7 @@
 F32 = jnp.float32
 BF16 = jnp.bfloat16
 NSEM = 160
+GATHER_ORDER = (1, 3, 2, 4, 5, 7, 6, 12, 13, 15, 14, 8, 9, 11, 10)
 PLANE_ORDER = (10, 6, 9, 11, 14, 5, 7, 13, 15, 2, 8, 1, 3, 4, 12)
 NT = (((1,), (1,)), ((), ()))
 MESH = pl.DeviceIdType.MESH
@@ -121,6 +122,7 @@
     for j in range(NCHUNK):
         copies[j].wait()
         m = mask[j]
+        adj[j] = m.astype(F32).astype(BF16)
         rowsum[...] += m[:, :128] + m[:, 128:]
         s = jnp.sum(m, axis=0, keepdims=True)
         colsum[0, 2 * j:2 * j + 1, :] = s[:, :128]
@@ -143,7 +145,7 @@
     def gather_plane(s):
         sems = stage_sem[s]['plane']
         ref = it.at[s, :, z, y, x]
-        for k in PLANE_ORDER:
+        for k in GATHER_ORDER:
             send(ref, ref, plane_peer((0, 2), k), plus(sems, k // SIDE))
         left(r2.at[s, 0], sems)
 
@@ -181,9 +183,9 @@
     scale_i[...] = lax.rsqrt(deg_i.astype(F32))
     for j in range(NCHUNK):
         su = scale_u[...]
-        m = mask[j].astype(F32)
-        adj[j, :, :128] = (su * m[:, :128] * scale_i[2 * j:2 * j + 1, :]).astype(BF16)
-        adj[j, :, 128:] = (su * m[:, 128:] * scale_i[2 * j + 1:2 * j + 2, :]).astype(BF16)
+        for l in range(2):
+            lanes = slice(128 * l, 128 * l + 128)
+            adj[j, :, lanes] = (su * scale_i[2 * j + l:2 * j + l + 1, :]).astype(BF16) * adj[j, :, lanes]
 
     def at(ref, axis, t):
         return ref.at[(slice(None),) * axis + (t,)]
@@ -291,18 +293,15 @@
     user_next(0)
     item_product(1, hold=True)
     scatter_mid(0)
-    for s in range(LAYERS):
-        if s == 0:
-            def late(i, _):
-                ky = lax.rem(i + 1, SIDE)
-                scatter_send(1, ky, lax.rem(y + ky, SIDE))
-                return 0
-            lax.fori_loop(0, SIDE, late, 0)
-        else:
-            gather_last(s)
-            user_own(s)
-            scatter_mid(s)
-            user_rest(s)
+
+    def late(i, _):
+        ky = lax.rem(i + 1, SIDE)
+        scatter_send(1, ky, lax.rem(y + ky, SIDE))
+        return 0
+
+    lax.fori_loop(0, SIDE, late, 0)
+
+    def item_next(s):
         new = scatter_end(s)
         for p in range(2):
             nxt = new[p].astype(BF16)
@@ -311,19 +310,25 @@
                 it[s + 1, p, z, y, x] = nxt
         if s + 1 < LAYERS:
             gather_plane(s + 1)
-        if s > 0:
-            user_there(s)
-            user_next(s)
-            if s + 1 < LAYERS:
-                item_product(s + 1)
+
+    item_next(0)
+    scatter_mid(1)
+    gather_last(1)
+    user_own(1)
+    item_next(1)
+    user_rest(1)
+    user_there(1)
+    user_next(1)
+    item_product(2)
+    gather_last(2)
+    user_own(2)
+    scatter_mid(2)
+    user_rest(2)
+    user_there(2)
+    user_next(2)
 
     tiles = n_batch // CHUNK
     iota = lax.broadcasted_iota(jnp.int32, (users, CHUNK), 0)
-    for p in range(2):
-        fin_b[p, x] = (i_acc[p] * 0.25).astype(BF16)
-    f_sem = fresh()
-    send_axis(2, lambda t: fin_b.at[:, x], lambda k: fin_b.at[:, x], f_sem)
-    left(fin_b.at[:, 0:3], f_sem)
     for h in range(2):
         ut[LAYERS, h] = (u_acc[h] * 0.25).astype(BF16)
     own_u = ut[LAYERS, col]
@@ -341,6 +346,12 @@
         picked = jnp.dot(own_u, hot, preferred_element_type=F32)
         for r in range(4):
             put_rows(r, t, picked[16 * r:16 * r + 16])
+    item_next(2)
+    for p in range(2):
+        fin_b[p, x] = (i_acc[p] * 0.25).astype(BF16)
+    f_sem = fresh()
+    send_axis(2, lambda t: fin_b.at[:, x], lambda k: fin_b.at[:, x], f_sem)
+    left(fin_b.at[:, 0:3], f_sem)
     base_i = (col * NCHUNK + z * SIDE + y) * CHUNK
     iota_i = lax.broadcasted_iota(jnp.int32, (CHUNK, CHUNK), 0)
     iota_b = lax.broadcasted_iota(jnp.int32, (128, CHUNK), 0)
@@ -412,21 +423,8 @@
     loss_ref[...] = jnp.sum(total, axis=1, keepdims=True) / n_batch
 
     iota2 = lax.broadcasted_iota(jnp.int32, (2 * users, CHUNK), 0)
-    prod_i[...] = jnp.zeros_like(prod_i)
+    s0 = LAYERS
     prod_u[...] = jnp.zeros_like(prod_u)
-    for t in range(tiles):
-        cut = slice(t * CHUNK, (t + 1) * CHUNK)
-        pos_hot = jnp.where(iota_i == ids_ref[1:2, cut] - base_i, 1.0, 0.0)
-        neg_hot = jnp.where(iota_i == ids_ref[2:3, cut] - base_i, 1.0, 0.0)
-        prod_i[...] += lax.dot_general(grad_i[:, cut], (pos_hot - neg_hot).astype(BF16), NT, preferred_element_type=F32)
-    seed = (prod_i[0:EMB, :] + prod_i[EMB:2 * EMB, :] + prod_i[2 * EMB:3 * EMB, :]) * 0.25
-    s0 = LAYERS
-    for part in range(2):
-        for q in range(SIDE):
-            block = seed[block_rows(part, q), block_lanes(q)]
-            s_item[part, q] = block
-            it[s0, part, z, y, q] = block.astype(BF16)
-    gather_line(s0)
     for t in range(tiles):
         cut = slice(t * CHUNK, (t + 1) * CHUNK)
         hot = jnp.where(iota2 == ids_ref[0:1, cut] - row * (2 * users), 1.0, 0.0).astype(BF16)
@@ -435,16 +433,39 @@
     for h in range(2):
         s_user[h] = seed[:, h * users:(h + 1) * users]
         ut[s0, h] = seed[:, h * users:(h + 1) * users].astype(BF16)
-
     item_product(s0)
+
+    def item_seeds(zz, _):
+        base = (col * NCHUNK + zz * SIDE + y) * CHUNK
+        prod_i[...] = jnp.zeros_like(prod_i)
+        for t in range(tiles):
+            cut = slice(t * CHUNK, (t + 1) * CHUNK)
+            pos_hot = jnp.where(iota_i == ids_ref[1:2, cut] - base, 1.0, 0.0)
+            neg_hot = jnp.where(iota_i == ids_ref[2:3, cut] - base, 1.0, 0.0)
+            prod_i[...] += lax.dot_general(grad_i[:, cut], (pos_hot - neg_hot).astype(BF16), NT, preferred_element_type=F32)
+        seed_i = (prod_i[0:EMB, :] + prod_i[EMB:2 * EMB, :] + prod_i[2 * EMB:3 * EMB, :]) * 0.25
+        for part in range(2):
+            for q in range(SIDE):
+                block = seed_i[block_rows(part, q), block_lanes(q)]
+                s_item[zz, part, q] = block
+                it[s0, part, zz, y, q] = block.astype(BF16)
+        ref = it.at[s0, :, zz, y]
+        for k in (1, 3, 2):
+            send(ref, ref, peer(1, k), plus(stage_sem[s0]['line'], k))
+        return 0
+
+    lax.fori_loop(0, SIDE, item_seeds, 0)
+    left(r1.at[s0, 0], stage_sem[s0]['line'])
+
     for s in range(s0, STAGES):
-        gather_last(s, line=s == s0)
+        if s > s0:
+            gather_last(s)
         user_own(s)
         scatter_mid(s)
         user_rest(s)
         new = scatter_end(s)
         for p in range(2):
-            nxt = s_item[p, x] + new[p]
+            nxt = s_item[z, p, x] + new[p]
             if s + 1 < STAGES:
                 it[s + 1, p, z, y, x] = nxt.astype(BF16)
             else:
@@ -493,7 +514,7 @@
             vm((S, EMB, EMB), BF16), vm((STAGES, 2, S, S, S) + tile, BF16), vm((STAGES, 2, S, S, S) + tile, F32),
             vm((STAGES, 2, S, S) + tile, F32),
             vm((STAGES, 2, S, 3, S) + tile, F32), vm((STAGES, 2, S * S - 1) + tile, F32),
-            vm((2,) + tile, F32), vm((2, S) + tile, F32),
+            vm((2,) + tile, F32), vm((S, 2, S) + tile, F32),
             vm((2, S) + tile, BF16), vm((2, S) + tile, F32), vm((CHUNK, EMB), F32),
             vm((2, 2, S, S, 3) + tile, BF16), vm((2, S, S, 3) + tile, BF16), vm((2, S, S, 3) + tile, BF16),
             vm((2, 3) + tile, BF16), vm((2, S * S - 1, 3) + tile, BF16), vm((2, 3, 3) + tile, BF16),

time: 140 us -> 136 us (0.971)
  Pallas kernels: 139 us -> 135 us
    pallas_call x1, Pallas kernels: 137 us -> 133 us  [local_fn(): pl.pallas_call(kernel, out_shape=outs, in_specs=[pl.BlockSpec(memory_spac...]
where the time goes in v4:
time: 136 us
  Pallas kernels  135 us (99%)
    pallas_call x1, Pallas kernels, local_fn(): pl.pallas_call(kernel, out_shape=outs, in_specs=[pl.BlockSpec(memory_spac...  133 us

profile of v4, /device:TPU:0, one launch (start us, length us, event | category | flops | bytes accessed | tf_op | source)
XLA Modules:
  0.0 136.1 jit_solution(7444626982054307538)
XLA Ops:
  0.6 133.3 %shard_map.83 = (bf16[64,256]{1,0:T(8,128)(2,1)}, bf16[64,64]{1,0:T(8,128)(2,1)}, f32[1,1]{1,0:T(1,128)}, f32[64,256]{1,0:T(8,128)}, f32[64,64]{1,0:T(8,128)}) custom-call(s32[512,4096]{1,0:T(8,128)} %mask_hbm.1, bf16[64,256]{1,0:T(8,128)(2,1)} %bitcast.5, bf16[64,64]{1,0:T(8,128)(2,1)} %item_ref.1, s32[3,2048]{1,0:T(4,128)} %bitcast.6), custom_call_target="tpu_custom_call" | custom-call | tf_op jit(solution)/shard_map/pallas_call | solution.py:527
  134.0 2.2 %shard_map.84 = (bf16[64,256]{1,0:T(8,128)(2,1)}, bf16[64,64]{1,0:T(8,128)(2,1)}, f32[1,1]{1,0:T(1,128)}, f32[64,256]{1,0:T(8,128)}, f32[64,64]{1,0:T(8,128)}) custom-call(bf16[64,256]{1,0:T(8,128)(2,1)} %get-tuple-element.15.refs_0_, bf16[64,64]{1,0:T(8,128)(2,1)} %get-tuple-element.16.refs_1_, f32[1,1]{1,0:T(1,128)} %get-tuple-element.17.refs_2_, ...), custom_call_target="tpu_custom_call" | custom-call | tf_op jit(solution)/shard_map/pallas_call | solution.py:536

commit v5 on v4

--- a/solution.py
+++ b/solution.py
@@ -259,13 +259,14 @@
         user_group(s, y, True)
 
     def user_rest(s):
-        def body(k, _):
+        def body(i, _):
+            k = 1 + lax.rem(2 * i, 3)
             yy = lax.rem(y + SIDE - k, SIDE)
             arrive(it.at[s, :, :, yy], plus(stage_sem[s]['line'], k))
             user_group(s, yy, False)
             return 0
 
-        lax.fori_loop(1, SIDE, body, 0)
+        lax.fori_loop(0, SIDE - 1, body, 0)
         sems = stage_sem[s]['user']
         send(up.at[s], up_in.at[s], partner, sems)
         left(up.at[s], sems)
@@ -312,9 +313,9 @@
             gather_plane(s + 1)
 
     item_next(0)
-    scatter_mid(1)
     gather_last(1)
     user_own(1)
+    scatter_mid(1)
     item_next(1)
     user_rest(1)
     user_there(1)
@@ -527,13 +528,14 @@
         fu, fi, loss, gu, gi = pl.pallas_call(
             kernel,
             out_shape=outs,
-            in_specs=[pl.BlockSpec(memory_space=pl.ANY), spec, spec, spec],
+            in_specs=[pl.BlockSpec(memory_space=pltpu.HBM), spec, spec, spec],
             out_specs=(spec,) * 5,
             scratch_shapes=scratch,
-            compiler_params=pltpu.CompilerParams(collective_id=0, has_side_effects=True, vmem_limit_bytes=56 * 1024 * 1024),
+            compiler_params=pltpu.CompilerParams(collective_id=0, has_side_effects=True, vmem_limit_bytes=52 * 1024 * 1024),
         )(mask_blk, user_emb.T, item_emb, triples.T)
         args = (fu, fi, loss, gu, gi)
-        fu, fi, loss, gu, gi = pl.pallas_call(hand_over, out_shape=outs, in_specs=[spec] * 5, out_specs=(spec,) * 5)(*args)
+        fu, fi, loss, gu, gi = pl.pallas_call(hand_over, out_shape=outs, in_specs=[spec] * 5, out_specs=(spec,) * 5,
+                                             compiler_params=pltpu.CompilerParams(vmem_limit_bytes=4 * 1024 * 1024))(*args)
         return fu.T, fi, loss[0, 0], gu.T, gi
 
     user_spec = P(('row', 'col'), None)

time: 136 us -> 139 us (1.022)
  local copies, waits for them, and re-layouts: 0 us -> 2.23 us
    unnamed x0 -> x6, local copies, waits for them, and re-layouts: none -> 2.23 us
where the time goes in v5:
time: 139 us; the launch traced here: 138 us
  Pallas kernels  135 us (97%)
  local copies, waits for them, and re-layouts  2.23 us (2%)
    pallas_call x1, Pallas kernels, local_fn(): pl.pallas_call(kernel, out_shape=outs, in_specs=[pl.BlockSpec(memory_spac...  134 us

profile of v5, /device:TPU:0, one launch (start us, length us, event | category | flops | bytes accessed | tf_op | source)
XLA Modules:
  0.0 138.3 jit_solution(2219157991918033000)
XLA Ops:
  0.6 0.0 copy-start
  0.6 0.7 copy-done
  1.4 0.0 copy-start.1
  1.4 0.8 copy-done.1
  2.1 0.0 copy-start.2
  2.2 0.7 copy-done.2
  2.9 134.2 %shard_map.83 = (bf16[64,256]{1,0:T(8,128)(2,1)S(1)}, bf16[64,64]{1,0:T(8,128)(2,1)S(1)}, f32[1,1]{1,0:T(1,128)}, f32[64,256]{1,0:T(8,128)S(1)}, f32[64,64]{1,0:T(8,128)S(1)}) custom-call(s32[512,4096]{1,0:T(8,128)} %mask_hbm.1, bf16[64,256]{1,0:T(8,128)(2,1)S(1)} %bitcast.5, bf16[64,64]{1,0:T(8,128)(2,1)S(1)} %copy-done.2, s32[3,2048]{1,0:T(4,128)S(1)} %bitcast.6), custom_call_target="tpu_custom_call" | custom-call | tf_op jit(solution)/shard_map/pallas_call | solution.py:528
  137.0 1.3 shard_map.84
Async XLA Ops:
  0.6 0.8 copy-start
  1.4 0.8 copy-start.1
  2.1 0.7 copy-start.2

commit v6 on v5

--- a/solution.py
+++ b/solution.py
@@ -37,14 +37,14 @@
     return jnp.concatenate(rows, axis=0)
 
 
-def kernel(mask_hbm, user_ref, item_ref, ids_ref,
+def kernel(mask_hbm, user_hbm, item_hbm, ids_hbm,
            fu_ref, fi_ref, loss_ref, gu_ref, gi_ref,
            mask, adj, rowsum, rowsum_in, scale_u, colsum, colsum_in, scale_i,
            ut, up, up_in, u_acc, s_user,
            nat, it, part_sum, q1, r1, r2, i_acc, s_item,
            fin_b, fin_f, nat_f,
            sel, sel_in, w0, w1, in1, in2, rows_all, grad_u, grad_i, prod_u, prod_i,
-           mask_sem, send_sem, recv_sem):
+           user_ref, item_ref, ids_ref, mask_sem, send_sem, recv_sem):
     row = lax.axis_index('row')
     col = lax.axis_index('col')
     pos = (lax.div(row, 16), lax.rem(lax.div(row, 4), 4), lax.rem(row, 4))
@@ -59,6 +59,11 @@
 
     partner = {'col': 1 - col}
 
+    small = []
+    for i, (src, dst) in enumerate(((user_hbm, user_ref), (item_hbm, item_ref), (ids_hbm, ids_ref))):
+        cp = pltpu.make_async_copy(src, dst, mask_sem.at[NCHUNK + i])
+        cp.start()
+        small.append(cp)
     copies = []
     for j in range(NCHUNK):
         cp = pltpu.make_async_copy(mask_hbm.at[:, pl.ds(j * CHUNK, CHUNK)], mask.at[j], mask_sem.at[j])
@@ -109,6 +114,8 @@
         for k in PLANE_ORDER:
             send(src(step[axes[0]][k // SIDE], step[axes[1]][k % SIDE]), dst(k - 1), plane_peer(axes, k), sems)
 
+    for cp in small:
+        cp.wait()
     ut[0, col] = user_ref[...]
     u_sem = fresh()
     send(ut.at[0, col], ut.at[0, col], partner, u_sem)
@@ -215,7 +222,7 @@
         send_axis(0, lambda t: part_sum.at[s, 0, t, yy], lambda k: r1.at[s, 0, ky, k], plus(sems[0], ky))
         send_axis(2, lambda t: part_sum.at[s, 1, :, yy, t], lambda k: r1.at[s, 1, ky, k], plus(sems[1], ky))
 
-    def scatter_mid(s):
+    def scatter_mid(s, between=None):
         sems = stage_sem[s]
 
         def piece(ky, yy, off, ks):
@@ -234,6 +241,8 @@
             return 0
 
         lax.fori_loop(1, SIDE, body, 0)
+        if between:
+            between()
         piece(0, y, 0, (2, 1, 3))
         for p in range(2):
             left(r2.at[s, p], sems['last'][p])
@@ -313,9 +322,8 @@
             gather_plane(s + 1)
 
     item_next(0)
-    gather_last(1)
+    scatter_mid(1, lambda: gather_last(1))
     user_own(1)
-    scatter_mid(1)
     item_next(1)
     user_rest(1)
     user_there(1)
@@ -522,20 +530,20 @@
             vm((2, 2, S, S, 3) + tile, BF16),
             vm((3 * EMB, n_b), BF16), vm((3 * EMB, n_b), BF16),
             vm((3 * EMB, n_u), F32), vm((3 * EMB, CHUNK), F32),
-            pltpu.SemaphoreType.DMA((NCHUNK,)), pltpu.SemaphoreType.DMA((NSEM,)), pltpu.SemaphoreType.DMA((NSEM,)),
+            vm((EMB, half), BF16), vm((EMB, EMB), BF16), vm((3, n_b), jnp.int32),
+            pltpu.SemaphoreType.DMA((NCHUNK + 3,)), pltpu.SemaphoreType.DMA((NSEM,)), pltpu.SemaphoreType.DMA((NSEM,)),
         ]
         spec = pl.BlockSpec(memory_space=pltpu.VMEM)
         fu, fi, loss, gu, gi = pl.pallas_call(
             kernel,
             out_shape=outs,
-            in_specs=[pl.BlockSpec(memory_space=pltpu.HBM), spec, spec, spec],
+            in_specs=[pl.BlockSpec(memory_space=pl.ANY)] * 4,
             out_specs=(spec,) * 5,
             scratch_shapes=scratch,
-            compiler_params=pltpu.CompilerParams(collective_id=0, has_side_effects=True, vmem_limit_bytes=52 * 1024 * 1024),
+            compiler_params=pltpu.CompilerParams(collective_id=0, has_side_effects=True, vmem_limit_bytes=56 * 1024 * 1024),
         )(mask_blk, user_emb.T, item_emb, triples.T)
         args = (fu, fi, loss, gu, gi)
-        fu, fi, loss, gu, gi = pl.pallas_call(hand_over, out_shape=outs, in_specs=[spec] * 5, out_specs=(spec,) * 5,
-                                             compiler_params=pltpu.CompilerParams(vmem_limit_bytes=4 * 1024 * 1024))(*args)
+        fu, fi, loss, gu, gi = pl.pallas_call(hand_over, out_shape=outs, in_specs=[spec] * 5, out_specs=(spec,) * 5)(*args)
         return fu.T, fi, loss[0, 0], gu.T, gi
 
     user_spec = P(('row', 'col'), None)

time: 139 us -> 133 us (0.957)
  Pallas kernels: 135 us -> 132 us
  local copies, waits for them, and re-layouts: 2.23 us -> 0 us
    pallas_call x1, Pallas kernels: 134 us -> 130 us  [local_fn(): pl.pallas_call(kernel, out_shape=outs, in_specs=[pl.BlockSpec(memory_spac...]
    unnamed x6 -> x0, local copies, waits for them, and re-layouts: 2.23 us -> none
where the time goes in v6:
time: 133 us
  Pallas kernels  132 us (99%)
    pallas_call x1, Pallas kernels, local_fn(): pl.pallas_call(kernel, out_shape=outs, in_specs=[pl.BlockSpec(memory_spac...  130 us

profile of v6, /device:TPU:0, one launch (start us, length us, event | category | flops | bytes accessed | tf_op | source)
XLA Modules:
  0.0 133.0 jit_solution(10645407762965312747)
XLA Ops:
  0.6 130.2 %shard_map.83 = (bf16[64,256]{1,0:T(8,128)(2,1)}, bf16[64,64]{1,0:T(8,128)(2,1)}, f32[1,1]{1,0:T(1,128)}, f32[64,256]{1,0:T(8,128)}, f32[64,64]{1,0:T(8,128)}) custom-call(s32[512,4096]{1,0:T(8,128)} %mask_hbm.1, bf16[64,256]{1,0:T(8,128)(2,1)} %bitcast.5, bf16[64,64]{1,0:T(8,128)(2,1)} %item_hbm.1, s32[3,2048]{1,0:T(4,128)} %bitcast.6), custom_call_target="tpu_custom_call" | custom-call | tf_op jit(solution)/shard_map/pallas_call | solution.py:537
  130.9 2.2 %shard_map.84 = (bf16[64,256]{1,0:T(8,128)(2,1)}, bf16[64,64]{1,0:T(8,128)(2,1)}, f32[1,1]{1,0:T(1,128)}, f32[64,256]{1,0:T(8,128)}, f32[64,64]{1,0:T(8,128)}) custom-call(bf16[64,256]{1,0:T(8,128)(2,1)} %get-tuple-element.15.refs_0_, bf16[64,64]{1,0:T(8,128)(2,1)} %get-tuple-element.16.refs_1_, f32[1,1]{1,0:T(1,128)} %get-tuple-element.17.refs_2_, ...), custom_call_target="tpu_custom_call" | custom-call | tf_op jit(solution)/shard_map/pallas_call | solution.py:546

commit v7 on v6

--- a/solution.py
+++ b/solution.py
@@ -43,7 +43,7 @@
            ut, up, up_in, u_acc, s_user,
            nat, it, part_sum, q1, r1, r2, i_acc, s_item,
            fin_b, fin_f, nat_f,
-           sel, sel_in, w0, w1, in1, in2, rows_all, grad_u, grad_i, prod_u, prod_i,
+           sel, sel_in, w0, w1, in1, in2, rows_all, grad_u, grad_i, prod_u, su, su_in, si, si_in, loss_out, loss_in,
            user_ref, item_ref, ids_ref, mask_sem, send_sem, recv_sem):
     row = lax.axis_index('row')
     col = lax.axis_index('col')
@@ -189,15 +189,15 @@
     deg_i = jnp.maximum(colsum[1] + jnp.sum(colsum_in[3:], axis=0), 1)
     scale_i[...] = lax.rsqrt(deg_i.astype(F32))
     for j in range(NCHUNK):
-        su = scale_u[...]
+        rowscale = scale_u[...]
         for l in range(2):
             lanes = slice(128 * l, 128 * l + 128)
-            adj[j, :, lanes] = (su * scale_i[2 * j + l:2 * j + l + 1, :]).astype(BF16) * adj[j, :, lanes]
+            adj[j, :, lanes] = (rowscale * scale_i[2 * j + l:2 * j + l + 1, :]).astype(BF16) * adj[j, :, lanes]
 
     def at(ref, axis, t):
         return ref.at[(slice(None),) * axis + (t,)]
 
-    def item_product(s, hold=False):
+    def item_product(s):
         lhs = jnp.concatenate([ut[s, 0], ut[s, 1]], axis=1)
 
         def body(i, _):
@@ -209,8 +209,7 @@
                 for part in range(2):
                     for q in range(SIDE):
                         part_sum[s, part, zz, yy, q] = out[block_rows(part, q), block_lanes(q)]
-            if not hold:
-                scatter_send(s, ky, yy)
+            scatter_send(s, ky, yy)
             return 0
 
         lax.fori_loop(0, SIDE, body, 0)
@@ -299,17 +298,10 @@
     item_product(0)
     user_own(0)
     user_rest(0)
+    scatter_mid(0)
     user_there(0)
     user_next(0)
-    item_product(1, hold=True)
-    scatter_mid(0)
-
-    def late(i, _):
-        ky = lax.rem(i + 1, SIDE)
-        scatter_send(1, ky, lax.rem(y + ky, SIDE))
-        return 0
-
-    lax.fori_loop(0, SIDE, late, 0)
+    item_product(1)
 
     def item_next(s):
         new = scatter_end(s)
@@ -406,15 +398,10 @@
         left(in1.at[p], sems3[p])
     for p in range(2):
         arrive(in1.at[p], sems3[p])
-    o_sem = fresh()
-    send(rows_all.at[col], rows_all.at[col], partner, o_sem)
-    left(rows_all.at[0], o_sem)
-    arrive(rows_all.at[1 - col], o_sem)
-
     total = jnp.zeros((1, 128), F32)
-    for lt in range(n_batch // 128):
+    for lt in range(n_batch // 256):
         def rows_of(group):
-            return jnp.concatenate([rows_all[lt // 8, (lt % 8) // 4, lt % 4, rt // 3, rt % 3].astype(F32)
+            return jnp.concatenate([rows_all[col, lt // 4, lt % 4, rt // 3, rt % 3].astype(F32)
                                     for rt in range(4 * group, 4 * group + 4)], axis=0)
         e_user, e_pos, e_neg = rows_of(0), rows_of(1), rows_of(2)
         margin = jnp.sum(e_user * e_pos, axis=0, keepdims=True) - jnp.sum(e_user * e_neg, axis=0, keepdims=True)
@@ -429,30 +416,63 @@
             ref[0:EMB, lanes] = hi
             ref[EMB:2 * EMB, lanes] = mid
             ref[2 * EMB:3 * EMB, lanes] = (low - mid.astype(F32)).astype(BF16)
-    loss_ref[...] = jnp.sum(total, axis=1, keepdims=True) / n_batch
+    loss_out[...] = jnp.broadcast_to(total, loss_out.shape)
+    l_sem = fresh()
+    send(loss_out, loss_in, partner, l_sem)
+    left(loss_out, l_sem)
 
     iota2 = lax.broadcasted_iota(jnp.int32, (2 * users, CHUNK), 0)
     s0 = LAYERS
+    own_half = pl.multiple_of(col * (n_batch // 2), 128)
+
+    def three(v):
+        return v[0:EMB] + v[EMB:2 * EMB] + v[2 * EMB:3 * EMB]
+
     prod_u[...] = jnp.zeros_like(prod_u)
-    for t in range(tiles):
+    for t in range(tiles // 2):
         cut = slice(t * CHUNK, (t + 1) * CHUNK)
-        hot = jnp.where(iota2 == ids_ref[0:1, cut] - row * (2 * users), 1.0, 0.0).astype(BF16)
+        ids = ids_ref[0:1, pl.ds(own_half + t * CHUNK, CHUNK)]
+        hot = jnp.where(iota2 == ids - row * (2 * users), 1.0, 0.0).astype(BF16)
         prod_u[...] += lax.dot_general(grad_u[:, cut], hot, NT, preferred_element_type=F32)
-    seed = (prod_u[0:EMB, :] + prod_u[EMB:2 * EMB, :] + prod_u[2 * EMB:3 * EMB, :]) * 0.25
+    seed = three(prod_u[...])
     for h in range(2):
-        s_user[h] = seed[:, h * users:(h + 1) * users]
-        ut[s0, h] = seed[:, h * users:(h + 1) * users].astype(BF16)
+        su[h] = seed[:, h * users:(h + 1) * users]
+    su_sem = fresh()
+    send(su, su_in, partner, su_sem)
+    left(su, su_sem)
+
+    def item_part(side, zz):
+        base = (side * NCHUNK + zz * SIDE + y) * CHUNK
+        acc = None
+        for t in range(tiles // 2):
+            cut = slice(t * CHUNK, (t + 1) * CHUNK)
+            at_t = pl.ds(own_half + t * CHUNK, CHUNK)
+            pos_hot = jnp.where(iota_i == ids_ref[1:2, at_t] - base, 1.0, 0.0)
+            neg_hot = jnp.where(iota_i == ids_ref[2:3, at_t] - base, 1.0, 0.0)
+            d = lax.dot_general(grad_i[:, cut], (pos_hot - neg_hot).astype(BF16), NT, preferred_element_type=F32)
+            acc = d if acc is None else acc + d
+        return three(acc)
+
+    si_sem = fresh(SIDE)
+
+    def other_seeds(zz, _):
+        si[zz] = item_part(1 - col, zz)
+        send(si.at[zz], si_in.at[zz], partner, plus(si_sem, zz))
+        return 0
+
+    lax.fori_loop(0, SIDE, other_seeds, 0)
+    left(si, si_sem)
+    arrive(su_in, su_sem)
+    for h in range(2):
+        v = (su[h] + su_in[h]) * 0.25
+        s_user[h] = v
+        ut[s0, h] = v.astype(BF16)
     item_product(s0)
 
     def item_seeds(zz, _):
-        base = (col * NCHUNK + zz * SIDE + y) * CHUNK
-        prod_i[...] = jnp.zeros_like(prod_i)
-        for t in range(tiles):
-            cut = slice(t * CHUNK, (t + 1) * CHUNK)
-            pos_hot = jnp.where(iota_i == ids_ref[1:2, cut] - base, 1.0, 0.0)
-            neg_hot = jnp.where(iota_i == ids_ref[2:3, cut] - base, 1.0, 0.0)
-            prod_i[...] += lax.dot_general(grad_i[:, cut], (pos_hot - neg_hot).astype(BF16), NT, preferred_element_type=F32)
-        seed_i = (prod_i[0:EMB, :] + prod_i[EMB:2 * EMB, :] + prod_i[2 * EMB:3 * EMB, :]) * 0.25
+        seed_i = item_part(col, zz)
+        arrive(si_in.at[zz], plus(si_sem, zz))
+        seed_i = (seed_i + si_in[zz]) * 0.25
         for part in range(2):
             for q in range(SIDE):
                 block = seed_i[block_rows(part, q), block_lanes(q)]
@@ -465,6 +485,8 @@
 
     lax.fori_loop(0, SIDE, item_seeds, 0)
     left(r1.at[s0, 0], stage_sem[s0]['line'])
+    arrive(loss_in, l_sem)
+    loss_ref[...] = jnp.sum(total + loss_in[0:1], axis=1, keepdims=True) / n_batch
 
     for s in range(s0, STAGES):
         if s > s0:
@@ -528,8 +550,9 @@
             vm((2, 2, S, S, 3) + tile, BF16), vm((2, S, S, 3) + tile, BF16), vm((2, S, S, 3) + tile, BF16),
             vm((2, 3) + tile, BF16), vm((2, S * S - 1, 3) + tile, BF16), vm((2, 3, 3) + tile, BF16),
             vm((2, 2, S, S, 3) + tile, BF16),
-            vm((3 * EMB, n_b), BF16), vm((3 * EMB, n_b), BF16),
-            vm((3 * EMB, n_u), F32), vm((3 * EMB, CHUNK), F32),
+            vm((3 * EMB, n_b // 2), BF16), vm((3 * EMB, n_b // 2), BF16),
+            vm((3 * EMB, n_u), F32), vm((2, EMB, half), F32), vm((2, EMB, half), F32),
+            vm((S, EMB, CHUNK), F32), vm((S, EMB, CHUNK), F32), vm((8, 128), F32), vm((8, 128), F32),
             vm((EMB, half), BF16), vm((EMB, EMB), BF16), vm((3, n_b), jnp.int32),
             pltpu.SemaphoreType.DMA((NCHUNK + 3,)), pltpu.SemaphoreType.DMA((NSEM,)), pltpu.SemaphoreType.DMA((NSEM,)),
         ]

time: 133 us -> 129 us (0.970)
  Pallas kernels: 132 us -> 128 us
    pallas_call x1, Pallas kernels: 130 us -> 126 us  [local_fn(): pl.pallas_call(kernel, out_shape=outs, in_specs=[pl.BlockSpec(memory_spac...]
where the time goes in v7:
time: 129 us
  Pallas kernels  128 us (99%)
    pallas_call x1, Pallas kernels, local_fn(): pl.pallas_call(kernel, out_shape=outs, in_specs=[pl.BlockSpec(memory_spac...  126 us

profile of v7, /device:TPU:0, one launch (start us, length us, event | category | flops | bytes accessed | tf_op | source)
XLA Modules:
  0.0 128.9 jit_solution(1897331155353349228)
XLA Ops:
  0.6 126.1 %shard_map.83 = (bf16[64,256]{1,0:T(8,128)(2,1)}, bf16[64,64]{1,0:T(8,128)(2,1)}, f32[1,1]{1,0:T(1,128)}, f32[64,256]{1,0:T(8,128)}, f32[64,64]{1,0:T(8,128)}) custom-call(s32[512,4096]{1,0:T(8,128)} %mask_hbm.1, bf16[64,256]{1,0:T(8,128)(2,1)} %bitcast.5, bf16[64,64]{1,0:T(8,128)(2,1)} %item_hbm.1, s32[3,2048]{1,0:T(4,128)} %bitcast.6), custom_call_target="tpu_custom_call" | custom-call | tf_op jit(solution)/shard_map/pallas_call | solution.py:560
  126.7 2.2 %shard_map.84 = (bf16[64,256]{1,0:T(8,128)(2,1)}, bf16[64,64]{1,0:T(8,128)(2,1)}, f32[1,1]{1,0:T(1,128)}, f32[64,256]{1,0:T(8,128)}, f32[64,64]{1,0:T(8,128)}) custom-call(bf16[64,256]{1,0:T(8,128)(2,1)} %get-tuple-element.15.refs_0_, bf16[64,64]{1,0:T(8,128)(2,1)} %get-tuple-element.16.refs_1_, f32[1,1]{1,0:T(1,128)} %get-tuple-element.17.refs_2_, ...), custom_call_target="tpu_custom_call" | custom-call | tf_op jit(solution)/shard_map/pallas_call | solution.py:569

commit v8 on v7

--- a/solution.py
+++ b/solution.py
@@ -188,16 +188,17 @@
     arrive(colsum_in.at[3:18], d_sem)
     deg_i = jnp.maximum(colsum[1] + jnp.sum(colsum_in[3:], axis=0), 1)
     scale_i[...] = lax.rsqrt(deg_i.astype(F32))
-    for j in range(NCHUNK):
+
+    def form(j):
         rowscale = scale_u[...]
         for l in range(2):
             lanes = slice(128 * l, 128 * l + 128)
-            adj[j, :, lanes] = (rowscale * scale_i[2 * j + l:2 * j + l + 1, :]).astype(BF16) * adj[j, :, lanes]
+            adj[j, :, lanes] = (rowscale * scale_i[pl.ds(2 * j + l, 1), :]).astype(BF16) * adj[j, :, lanes]
 
     def at(ref, axis, t):
         return ref.at[(slice(None),) * axis + (t,)]
 
-    def item_product(s):
+    def item_product(s, before=None):
         lhs = jnp.concatenate([ut[s, 0], ut[s, 1]], axis=1)
 
         def body(i, _):
@@ -205,6 +206,8 @@
             yy = lax.rem(y + ky, SIDE)
             for kz in (2, 1, 3, 0):
                 zz = step[0][kz]
+                if before:
+                    before(zz * SIDE + yy)
                 out = jnp.dot(lhs, adj[zz * SIDE + yy], preferred_element_type=F32)
                 for part in range(2):
                     for q in range(SIDE):
@@ -295,7 +298,7 @@
             if s + 1 < LAYERS:
                 ut[s + 1, h] = nxt
 
-    item_product(0)
+    item_product(0, form)
     user_own(0)
     user_rest(0)
     scatter_mid(0)

time: 129 us -> 130 us (level)
  no operation moved by 1% of the time
where the time goes in v8:
time: 130 us
  Pallas kernels  129 us (99%)
    pallas_call x1, Pallas kernels, local_fn(): pl.pallas_call(kernel, out_shape=outs, in_specs=[pl.BlockSpec(memory_spac...  127 us

profile of v8, /device:TPU:0, one launch (start us, length us, event | category | flops | bytes accessed | tf_op | source)
XLA Modules:
  0.0 129.9 jit_solution(14348434319401487098)
XLA Ops:
  0.6 127.1 %shard_map.83 = (bf16[64,256]{1,0:T(8,128)(2,1)}, bf16[64,64]{1,0:T(8,128)(2,1)}, f32[1,1]{1,0:T(1,128)}, f32[64,256]{1,0:T(8,128)}, f32[64,64]{1,0:T(8,128)}) custom-call(s32[512,4096]{1,0:T(8,128)} %mask_hbm.1, bf16[64,256]{1,0:T(8,128)(2,1)} %bitcast.5, bf16[64,64]{1,0:T(8,128)(2,1)} %item_hbm.1, s32[3,2048]{1,0:T(4,128)} %bitcast.6), custom_call_target="tpu_custom_call" | custom-call | tf_op jit(solution)/shard_map/pallas_call | solution.py:563
  127.7 2.2 %shard_map.84 = (bf16[64,256]{1,0:T(8,128)(2,1)}, bf16[64,64]{1,0:T(8,128)(2,1)}, f32[1,1]{1,0:T(1,128)}, f32[64,256]{1,0:T(8,128)}, f32[64,64]{1,0:T(8,128)}) custom-call(bf16[64,256]{1,0:T(8,128)(2,1)} %get-tuple-element.15.refs_0_, bf16[64,64]{1,0:T(8,128)(2,1)} %get-tuple-element.16.refs_1_, f32[1,1]{1,0:T(1,128)} %get-tuple-element.17.refs_2_, ...), custom_call_target="tpu_custom_call" | custom-call | tf_op jit(solution)/shard_map/pallas_call | solution.py:572

commit v9 on v7

--- a/solution.py
+++ b/solution.py
@@ -338,7 +338,7 @@
     def put_rows(rt, t, picked):
         for l in range(2):
             lt = 2 * t + l
-            sel[lt // 8, (lt % 8) // 4, lt % 4, rt // 3, rt % 3] = picked[:, 128 * l:128 * l + 128].astype(BF16)
+            sel[lt // 8, rt % 3, lt % 4, rt // 3, (lt % 8) // 4] = picked[:, 128 * l:128 * l + 128].astype(BF16)
 
     base_u = (2 * row + col) * users
     for t in range(tiles):
@@ -373,35 +373,35 @@
     left(sel_in, x_sem)
     arrive(sel_in, x_sem)
     w0[...] = sel[col] + sel_in[...]
-    ax0, ax2 = (0, 2), (2, 0)
-    sems = [fresh() for _ in range(2)]
-    for p in range(2):
-        send_plane((ax0[p], 1), lambda t0, t1: w0.at[p, t0, t1], lambda k: in1.at[p, k], sems[p])
+    planes, third = ((0, 1), (2, 1), (0, 2)), (2, 0, 1)
+    sems = [fresh() for _ in range(3)]
+    for p in range(3):
+        send_plane(planes[p], lambda t0, t1: w0.at[p, t0, t1], lambda k: in1.at[p, k], sems[p])
         left(in1.at[p], sems[p])
     arrive(fin_b.at[:, 0:3], f_sem)
     nat_f[...] = join_blocks(lambda part, q: fin_b[part, q]).astype(F32).T
     own = pl.ds(pl.multiple_of(x * EMB, EMB), EMB)
     fi_ref[...] = nat_f[own, :].astype(BF16)
-    sems2 = [fresh() for _ in range(2)]
-    for p in range(2):
+    sems2 = [fresh() for _ in range(3)]
+    for p in range(3):
         arrive(in1.at[p], sems[p])
-        w1[p] = (w0[p, pos[ax0[p]], y].astype(F32) + jnp.sum(in1[p].astype(F32), axis=0)).astype(BF16)
-        send_axis(ax2[p], lambda t: w1.at[p], lambda k: in2.at[p, k], sems2[p])
+        mine = w0[p, pos[planes[p][0]], pos[planes[p][1]]].astype(F32)
+        w1[p] = (mine + jnp.sum(in1[p].astype(F32), axis=0)).astype(BF16)
+        send_axis(third[p], lambda t: w1.at[p], lambda k: in2.at[p, k], sems2[p])
         left(in2.at[p], sems2[p])
-    sems3 = [fresh() for _ in range(2)]
-    for p in range(2):
+    sems3 = [fresh() for _ in range(3)]
+    for p in range(3):
         arrive(in2.at[p], sems2[p])
-        a = pos[ax0[p]]
-        rows_all[col, p, a, y] = w1[p] + in2[p, 0] + in2[p, 1] + in2[p, 2]
-        ref = rows_all.at[col, p, a, y]
-        send_plane((ax0[p], 1), lambda t0, t1: ref, lambda k: ref, sems3[p])
+        ref = rows_all.at[col, p, pos[planes[p][0]], pos[planes[p][1]]]
+        ref[...] = w1[p] + in2[p, 0] + in2[p, 1] + in2[p, 2]
+        send_plane(planes[p], lambda t0, t1: ref, lambda k: ref, sems3[p])
         left(in1.at[p], sems3[p])
-    for p in range(2):
+    for p in range(3):
         arrive(in1.at[p], sems3[p])
     total = jnp.zeros((1, 128), F32)
     for lt in range(n_batch // 256):
         def rows_of(group):
-            return jnp.concatenate([rows_all[col, lt // 4, lt % 4, rt // 3, rt % 3].astype(F32)
+            return jnp.concatenate([rows_all[col, rt % 3, lt % 4, rt // 3, lt // 4].astype(F32)
                                     for rt in range(4 * group, 4 * group + 4)], axis=0)
         e_user, e_pos, e_neg = rows_of(0), rows_of(1), rows_of(2)
         margin = jnp.sum(e_user * e_pos, axis=0, keepdims=True) - jnp.sum(e_user * e_neg, axis=0, keepdims=True)
@@ -547,9 +547,9 @@
             vm((STAGES, 2, S, 3, S) + tile, F32), vm((STAGES, 2, S * S - 1) + tile, F32),
             vm((2,) + tile, F32), vm((S, 2, S) + tile, F32),
             vm((2, S) + tile, BF16), vm((2, S) + tile, F32), vm((CHUNK, EMB), F32),
-            vm((2, 2, S, S, 3) + tile, BF16), vm((2, S, S, 3) + tile, BF16), vm((2, S, S, 3) + tile, BF16),
-            vm((2, 3) + tile, BF16), vm((2, S * S - 1, 3) + tile, BF16), vm((2, 3, 3) + tile, BF16),
-            vm((2, 2, S, S, 3) + tile, BF16),
+            vm((2, 3, S, S, 2) + tile, BF16), vm((3, S, S, 2) + tile, BF16), vm((3, S, S, 2) + tile, BF16),
+            vm((3, 2) + tile, BF16), vm((3, S * S - 1, 2) + tile, BF16), vm((3, 3, 2) + tile, BF16),
+            vm((2, 3, S, S, 2) + tile, BF16),
             vm((3 * EMB, n_b // 2), BF16), vm((3 * EMB, n_b // 2), BF16),
             vm((3 * EMB, n_u), F32), vm((2, EMB, half), F32), vm((2, EMB, half), F32),
             vm((S, EMB, CHUNK), F32), vm((S, EMB, CHUNK), F32), vm((8, 128), F32), vm((8, 128), F32),

time: 129 us -> 128 us (level)
    pallas_call x1, Pallas kernels: 126 us -> 125 us  [local_fn(): pl.pallas_call(kernel, out_shape=outs, in_specs=[pl.BlockSpec(memory_spac...]
where the time goes in v9:
time: 128 us; the launch traced here: 127 us
  Pallas kernels  127 us (99%)
    pallas_call x1, Pallas kernels, local_fn(): pl.pallas_call(kernel, out_shape=outs, in_specs=[pl.BlockSpec(memory_spac...  125 us

profile of v9, /device:TPU:0, one launch (start us, length us, event | category | flops | bytes accessed | tf_op | source)
XLA Modules:
  0.0 127.3 jit_solution(10526359742803762874)
XLA Ops:
  0.6 124.5 %shard_map.83 = (bf16[64,256]{1,0:T(8,128)(2,1)}, bf16[64,64]{1,0:T(8,128)(2,1)}, f32[1,1]{1,0:T(1,128)}, f32[64,256]{1,0:T(8,128)}, f32[64,64]{1,0:T(8,128)}) custom-call(s32[512,4096]{1,0:T(8,128)} %mask_hbm.1, bf16[64,256]{1,0:T(8,128)(2,1)} %bitcast.5, bf16[64,64]{1,0:T(8,128)(2,1)} %item_hbm.1, s32[3,2048]{1,0:T(4,128)} %bitcast.6), custom_call_target="tpu_custom_call" | custom-call | tf_op jit(solution)/shard_map/pallas_call | solution.py:560
  125.2 2.2 %shard_map.84 = (bf16[64,256]{1,0:T(8,128)(2,1)}, bf16[64,64]{1,0:T(8,128)(2,1)}, f32[1,1]{1,0:T(1,128)}, f32[64,256]{1,0:T(8,128)}, f32[64,64]{1,0:T(8,128)}) custom-call(bf16[64,256]{1,0:T(8,128)(2,1)} %get-tuple-element.15.refs_0_, bf16[64,64]{1,0:T(8,128)(2,1)} %get-tuple-element.16.refs_1_, f32[1,1]{1,0:T(1,128)} %get-tuple-element.17.refs_2_, ...), custom_call_target="tpu_custom_call" | custom-call | tf_op jit(solution)/shard_map/pallas_call | solution.py:569

commit v10 on v9

--- a/solution.py
+++ b/solution.py
@@ -134,11 +134,14 @@
         s = jnp.sum(m, axis=0, keepdims=True)
         colsum[0, 2 * j:2 * j + 1, :] = s[:, :128]
         colsum[0, 2 * j + 1:2 * j + 2, :] = s[:, 128:]
-    r_sem, c_sem = fresh(), fresh()
+    r_sem = fresh()
+    parts = ((slice(0, 16), 0, (1, 2)), (slice(16, 24), 2, (1, 0)), (slice(24, 32), 1, (0, 2)))
+    c_sem = [fresh() for _ in parts]
     send(rowsum, rowsum_in, partner, r_sem)
     left(rowsum, r_sem)
-    send_axis(0, lambda t: colsum.at[0], lambda k: colsum_in.at[k], c_sem)
-    left(colsum_in.at[0:3], c_sem)
+    for (rows, axis, _), sems in zip(parts, c_sem):
+        send_axis(axis, lambda t: colsum.at[0, rows], lambda k: colsum_in.at[k, rows], sems)
+        left(colsum_in.at[0:3, rows], sems)
 
     arrive(nat.at[0:3], n_sem)
     chunk0 = jnp.concatenate([nat[k].astype(F32) for k in range(SIDE)], axis=0).T
@@ -179,13 +182,15 @@
     arrive(rowsum_in, r_sem)
     deg_u = jnp.maximum(jnp.sum(rowsum[...] + rowsum_in[...], axis=1, keepdims=True), 1)
     scale_u[...] = jnp.broadcast_to(lax.rsqrt(deg_u.astype(F32)), scale_u.shape)
-    arrive(colsum_in.at[0:3], c_sem)
-    colsum[1] = colsum[0] + colsum_in[0] + colsum_in[1] + colsum_in[2]
-    d_sem = fresh()
-    send_plane((1, 2), lambda t0, t1: colsum.at[1], lambda k: colsum_in.at[3 + k], d_sem)
-    left(colsum_in.at[3:18], d_sem)
+    d_sem = [fresh() for _ in parts]
+    for (rows, _, axes), sems, sems2 in zip(parts, c_sem, d_sem):
+        arrive(colsum_in.at[0:3, rows], sems)
+        colsum[1, rows] = colsum[0, rows] + colsum_in[0, rows] + colsum_in[1, rows] + colsum_in[2, rows]
+        send_plane(axes, lambda t0, t1: colsum.at[1, rows], lambda k: colsum_in.at[3 + k, rows], sems2)
+        left(colsum_in.at[3:18, rows], sems2)
     gather_last(0, line=True)
-    arrive(colsum_in.at[3:18], d_sem)
+    for (rows, _, _), sems in zip(parts, d_sem):
+        arrive(colsum_in.at[3:18, rows], sems)
     deg_i = jnp.maximum(colsum[1] + jnp.sum(colsum_in[3:], axis=0), 1)
     scale_i[...] = lax.rsqrt(deg_i.astype(F32))
     for j in range(NCHUNK):

time: 128 us -> 127 us (level)
  no operation moved by 1% of the time
where the time goes in v10:
time: 127 us
  Pallas kernels  126 us (99%)
    pallas_call x1, Pallas kernels, local_fn(): pl.pallas_call(kernel, out_shape=outs, in_specs=[pl.BlockSpec(memory_spac...  124 us

profile of v10, /device:TPU:0, one launch (start us, length us, event | category | flops | bytes accessed | tf_op | source)
XLA Modules:
  0.0 127.1 jit_solution(12072098778985859873)
XLA Ops:
  0.6 124.3 %shard_map.83 = (bf16[64,256]{1,0:T(8,128)(2,1)}, bf16[64,64]{1,0:T(8,128)(2,1)}, f32[1,1]{1,0:T(1,128)}, f32[64,256]{1,0:T(8,128)}, f32[64,64]{1,0:T(8,128)}) custom-call(s32[512,4096]{1,0:T(8,128)} %mask_hbm.1, bf16[64,256]{1,0:T(8,128)(2,1)} %bitcast.5, bf16[64,64]{1,0:T(8,128)(2,1)} %item_hbm.1, s32[3,2048]{1,0:T(4,128)} %bitcast.6), custom_call_target="tpu_custom_call" | custom-call | tf_op jit(solution)/shard_map/pallas_call | solution.py:565
  124.9 2.2 %shard_map.84 = (bf16[64,256]{1,0:T(8,128)(2,1)}, bf16[64,64]{1,0:T(8,128)(2,1)}, f32[1,1]{1,0:T(1,128)}, f32[64,256]{1,0:T(8,128)}, f32[64,64]{1,0:T(8,128)}) custom-call(bf16[64,256]{1,0:T(8,128)(2,1)} %get-tuple-element.15.refs_0_, bf16[64,64]{1,0:T(8,128)(2,1)} %get-tuple-element.16.refs_1_, f32[1,1]{1,0:T(1,128)} %get-tuple-element.17.refs_2_, ...), custom_call_target="tpu_custom_call" | custom-call | tf_op jit(solution)/shard_map/pallas_call | solution.py:574
